TPU v7x, 512 devices: a whole 4x4x16 slice. The times are simulated.
512 devices in a mesh: dp: 64 (over y, z), tensor: 8 (over x, core).
Axes of the slice: x: 4, y: 4, z: 16, core: 2. Of those that a mesh axis runs over, the one named last changes fastest.
Arguments:
- inputs: bfloat16 [36864, 8192], P('dp', 'tensor'), may hold values from -6 to 6
- out_grads: bfloat16 [36864, 11264], P('dp', 'tensor'), may hold values from -600 to 600
- basis: bfloat16 [8192, 512], P('dp', 'tensor'), may hold values from -40 to 40
- weight: bfloat16 [8192, 11264], P('dp', 'tensor'), may hold values from -0.099609375 to 0.099609375
- first_moment: float32 [512, 11264], P('dp', 'tensor'), may hold values from -0.9 to 0.9
- second_moment: float32 [512, 11264], P('dp', 'tensor'), may hold values from 0.01 to 1
Outputs:
- new_weight: bfloat16 [8192, 11264], P('dp', 'tensor')
- new_first: float32 [512, 11264], P('dp', 'tensor')
- new_second: float32 [512, 11264], P('dp', 'tensor')
All inputs are finite; a program needn't handle non-finite values.
Results may differ from a plain program's by a relative error of at most 0.0087.
Values may be sent and summed in bfloat16 or wider, within the bound.
No kernel may reach another device: no remote copies, remote signals or barrier semaphores. Data moves between devices by JAX's collectives and lax.ppermute only.
A program may use at most 64 MiB of HBM per device.

v0:
```python
import math

import jax
import jax.numpy as jnp
from jax import lax
from jax.sharding import Mesh
from jax.sharding import PartitionSpec as P

FW = 11264
R = 512
DP = ("dp_0", "dp_1")
TENSOR = ("tensor_0", "tensor_1")


beta_one = 0.9
beta_two = 0.999
adam_eps = 1e-08
corr_one = 1.0 - 0.9**10
corr_two = 1.0 - 0.999**10
step_size = 0.002
decay_keep = 0.99


def in_order(pieces, dim):
    shape = list(pieces.shape[1:])
    shape[dim] *= pieces.shape[0]
    return jnp.moveaxis(pieces, 0, dim).reshape(shape)


def stacked_from(x, axes, sequence):
    pieces = x
    for k in sequence:
        pieces = lax.all_gather(pieces, axes[k])
    done = sequence[::-1]
    back = [done.index(k) for k in range(len(axes))]
    pieces = pieces.transpose(*back, *range(len(axes), pieces.ndim))
    return pieces.reshape(-1, *x.shape)


def gathered_by_axis(x, axes, sequence, dim):
    return in_order(stacked_from(x, axes, sequence), dim)


def sent_to_all(x, axis):
    copies = jnp.broadcast_to(x, (lax.axis_size(axis), *x.shape))
    return lax.all_to_all(copies, axis, split_axis=0, concat_axis=0, tiled=True)


def taken_together(x, axis):
    everything = sent_to_all(x, axis)
    return jnp.sum(everything.astype(jnp.float32), axis=0)


def in_blocks(x, dim, length):
    shape = x.shape
    pieces = x.reshape(*shape[:dim], length, shape[dim] // length, *shape[dim + 1 :])
    return jnp.moveaxis(pieces, dim, 0)


def sum_at_owner(x, axis, dim):
    pieces = in_blocks(x, dim, lax.axis_size(axis))
    arrived = lax.all_to_all(pieces, axis, split_axis=0, concat_axis=0, tiled=True)
    return arrived.astype(jnp.float32).sum(axis=0)


def over_copies(x, axis):
    everything = sent_to_all(x, axis)
    return jnp.sum(everything, axis=0)


def by_axis(x, axes):
    far, near = axes
    return over_copies(over_copies(x, near), far)


def gather_directly(x, axis, dim):
    pieces = sent_to_all(x, axis)
    return in_order(pieces, dim)


def adam_update(lowrank, square, first_moment, second_moment):
    bound_norm = math.sqrt(R * FW)
    factor = jnp.minimum(1.0, bound_norm / (jnp.sqrt(square) + 1e-06))
    clipped = lowrank * factor
    first = beta_one * first_moment + (1.0 - beta_one) * clipped
    second = beta_two * second_moment + (1.0 - beta_two) * clipped * clipped
    update = (first / corr_one / (jnp.sqrt(second / corr_two) + adam_eps)).astype(jnp.bfloat16)
    return (first, second, update)


def on_device(inputs, out_grads, basis, weight, first_moment, second_moment):
    columns = gathered_by_axis(basis, DP, (0, 1), 0)
    regrouped = lax.all_to_all(columns, TENSOR, split_axis=0, concat_axis=1, tiled=True)
    partial_value = jnp.dot(inputs, regrouped, preferred_element_type=jnp.float32)
    projected = (
        taken_together(partial_value.astype(jnp.bfloat16), TENSOR)
        .astype(jnp.float32)
        .astype(jnp.bfloat16)
    )
    partial_low = lax.dot_general(
        projected, out_grads, (((0,), (0,)), ((), ())), preferred_element_type=jnp.float32
    )
    own_rows = sum_at_owner(partial_low.astype(jnp.bfloat16), DP, 0)
    square = by_axis(jnp.sum(own_rows * own_rows), (("dp_0", "dp_1"), ("tensor_0", "tensor_1")))
    first, second, update = adam_update(own_rows, square, first_moment, second_moment)
    back_basis = gather_directly(basis, TENSOR, 1)
    delta = jnp.dot(
        back_basis, gathered_by_axis(update, DP, (0, 1), 0), preferred_element_type=jnp.float32
    )
    new_weight = (decay_keep * weight.astype(jnp.float32) - step_size * delta).astype(jnp.bfloat16)
    return (new_weight, first, second)


def solution(mesh):
    torus = Mesh(mesh.devices.reshape(4, 16, 4, 2), ("dp_0", "dp_1", "tensor_0", "tensor_1"))
    return jax.shard_map(
        on_device,
        mesh=torus,
        in_specs=(
            P(DP, TENSOR),
            P(DP, TENSOR),
            P(DP, TENSOR),
            P(DP, TENSOR),
            P(DP, TENSOR),
            P(DP, TENSOR),
        ),
        out_specs=(P(DP, TENSOR), P(DP, TENSOR), P(DP, TENSOR)),
        check_vma=False,
    )
```

profile of v0, /device:TPU:6, one launch (start us, length us, event | category | flops | bytes accessed | tf_op | source)
XLA Modules:
  0.0 383.0 jit_solution(8275225090253299334)
XLA Ops:
  7.2 0.0 all-gather.7.cloned.1.call-start
  7.2 11.7 %all-gather = bf16[512,64]{0,1:T(8,128)(2,1)S(1)} all-gather(bf16[128,64]{0,1:T(8,128)(2,1)} %param.8), channel_id=2, replica_groups=mesh['dp_0'=4,'dp_1'=16,'tensor_0'=4,'tensor_1'=2] {'dp_0'}, dimensions={0}, use_global_device_ids=true | all-gather | bytes 81920 | tf_op jit(solution)/shard_map/all_gather | solution.py:33
  18.9 0.6 copy_bitcast_fusion
  19.5 0.0 all-gather.9.cloned.1.call-start
  19.6 74.2 %all-gather.7.cloned.1.call-done = bf16[64,128,64]{1,2,0:T(8,128)(2,1)} async-done(((bf16[4,128,64]{1,2,0:T(8,128)(2,1)}), bf16[64,128,64]{1,2,0:T(8,128)(2,1)}) %all-gather.7.cloned.1.call-update) | async-done | bytes 1048592 | tf_op jit(solution)/shard_map/all_gather | solution.py:33
  93.8 1.9 copy.40
  95.7 1.3 all_to_all.31
  97.0 1.8 copy.41
  98.8 18.6 %all_to_all.46 = bf16[8,1024,64]{1,2,0:T(8,128)(2,1)S(1)} all-to-all(bf16[8,1024,64]{1,2,0:T(8,128)(2,1)S(1)} %copy.41), channel_id=1, replica_groups=mesh['dp_0'=4,'dp_1'=16,'tensor_0'=4,'tensor_1'=2] {'tensor_0','tensor_1'}, dimensions={0} | all-to-all | bytes 2097152 | tf_op jit(solution)/shard_map/all_to_all | solution.py:93
  117.4 0.8 convolution_convert_fusion.1
  118.3 0.4 broadcast_in_dim.12
  118.7 58.6 %all_to_all.47 = bf16[8,576,512]{2,1,0:T(8,128)(2,1)} all-to-all(bf16[8,576,512]{2,1,0:T(8,128)(2,1)S(1)} %broadcast_in_dim.12), channel_id=1, replica_groups=mesh['dp_0'=4,'dp_1'=16,'tensor_0'=4,'tensor_1'=2] {'tensor_0','tensor_1'}, dimensions={0} | all-to-all | bytes 9437184 | tf_op jit(solution)/shard_map/all_to_all | solution.py:46
  177.2 3.3 reduce_sum.48
  180.6 1.4 fusion
  182.0 81.2 %all_to_all.48 = bf16[64,8,1408]{2,1,0:T(8,128)(2,1)S(1)} all-to-all(bf16[64,8,1408]{2,1,0:T(8,128)(2,1)S(1)} %fusion), channel_id=1, replica_groups=mesh['dp_0'=4,'dp_1'=16,'tensor_0'=4,'tensor_1'=2] {'dp_0','dp_1'}, dimensions={0} | all-to-all | bytes 2883584 | tf_op jit(solution)/shard_map/all_to_all | solution.py:62
  263.2 0.2 convert_reduce_fusion
  263.4 0.6 multiply_reduce_fusion
  264.0 0.6 broadcast_in_dim.13
  264.7 7.9 %all_to_all.49 = f32[8,1,1]{2,1,0:T(1,128)S(1)} all-to-all(f32[8,1,1]{2,1,0:T(1,128)S(1)} %broadcast_in_dim.13), channel_id=1, replica_groups=mesh['dp_0'=4,'dp_1'=16,'tensor_0'=4,'tensor_1'=2] {'tensor_0','tensor_1'}, dimensions={0} | all-to-all | bytes 64 | tf_op jit(solution)/shard_map/all_to_all | solution.py:46
  272.6 0.6 reduce_sum.51
  273.2 0.7 broadcast_in_dim.14
  273.8 21.3 %all_to_all.50 = f32[64,1,1]{2,1,0:T(1,128)S(1)} all-to-all(f32[64,1,1]{2,1,0:T(1,128)S(1)} %broadcast_in_dim.14), channel_id=1, replica_groups=mesh['dp_0'=4,'dp_1'=16,'tensor_0'=4,'tensor_1'=2] {'dp_0','dp_1'}, dimensions={0} | all-to-all | bytes 512 | tf_op jit(solution)/shard_map/all_to_all | solution.py:46
  295.1 0.7 reduce_sum.52
  296.5 0.7 divide_convert_fusion
  297.2 12.7 %all-gather.2 = bf16[32,1408]{1,0:T(8,128)(2,1)} all-gather(bf16[8,1408]{1,0:T(8,128)(2,1)S(1)} %get-tuple-element.24), channel_id=4, replica_groups=mesh['dp_0'=4,'dp_1'=16,'tensor_0'=4,'tensor_1'=2] {'dp_0'}, dimensions={0}, use_global_device_ids=true | all-gather | bytes 112640 | tf_op jit(solution)/shard_map/all_gather | solution.py:33
  309.9 0.7 broadcast_in_dim.15
  310.6 5.4 %all-to-all-start.5 = ((bf16[8,128,64]{1,2,0:T(8,128)(2,1)}), bf16[8,128,64]{1,2,0:T(8,128)(2,1)S(1)}, u32[]{:S(2)}, u32[]{:S(2)}) async-start(bf16[8,128,64]{1,2,0:T(8,128)(2,1)} %broadcast_in_dim.15), calls=%async_computation.5 | async-start | bytes 262144 | tf_op jit(solution)/shard_map/all_to_all | solution.py:46
  315.9 0.2 copy.38
  316.2 55.3 %all-gather.9.cloned.1.call-done = bf16[64,8,1408]{2,1,0:T(8,128)(2,1)} async-done(((bf16[4,8,1408]{2,1,0:T(8,128)(2,1)}), bf16[64,8,1408]{2,1,0:T(8,128)(2,1)}) %all-gather.9.cloned.1.call-update) | async-done | bytes 1441808 | tf_op jit(solution)/shard_map/all_gather | solution.py:33
  371.4 1.5 copy.44
  372.9 1.3 fusion.3
  374.2 1.9 copy.45
  (15 shorter events, 0.1 us)
Async XLA Ops:
  7.2 173.4 %copy-start = (bf16[576,1408]{1,0:T(8,128)(2,1)S(1)}, bf16[576,1408]{1,0:T(8,128)(2,1)}, u32[]{:S(2)}) copy-start(bf16[576,1408]{1,0:T(8,128)(2,1)} %param.7) | copy-start | bytes 4866052
  7.2 86.6 %all-gather.7.cloned.1.call-start = ((), (), s32[]{:S(2)}) async-start(), calls=%async_computation.6 | async-start | bytes 1114112 | tf_op jit(solution)/shard_map/all_gather | solution.py:33
  19.5 351.9 %all-gather.9.cloned.1.call-start = ((), (), s32[]{:S(2)}) async-start(), calls=%async_computation.7 | async-start | bytes 1531904 | tf_op jit(solution)/shard_map/all_gather | solution.py:33
  98.8 18.6 %copy-start.5 = (bf16[576,1024]{1,0:T(8,128)(2,1)S(1)}, bf16[576,1024]{1,0:T(8,128)(2,1)}, u32[]{:S(2)}) copy-start(bf16[576,1024]{1,0:T(8,128)(2,1)} %param.6) | copy-start | bytes 3538948
  263.2 33.3 %copy-start.3 = (f32[8,1408]{1,0:T(8,128)S(1)}, f32[8,1408]{1,0:T(8,128)}, u32[]{:S(2)}) copy-start(f32[8,1408]{1,0:T(8,128)} %param.10) | copy-start | bytes 135172
  263.2 33.3 %copy-start.4 = (f32[8,1408]{1,0:T(8,128)S(1)}, f32[8,1408]{1,0:T(8,128)}, u32[]{:S(2)}) copy-start(f32[8,1408]{1,0:T(8,128)} %param.11) | copy-start | bytes 135172
  263.2 46.7 %copy-start.2 = (bf16[128,64]{0,1:T(8,128)(2,1)S(1)}, bf16[128,64]{0,1:T(8,128)(2,1)}, u32[]{:S(2)}) copy-start(bf16[128,64]{0,1:T(8,128)(2,1)} %param.8) | copy-start | bytes 49156
  263.2 52.8 %copy-start.1 = (bf16[128,1408]{1,0:T(8,128)(2,1)S(1)}, bf16[128,1408]{1,0:T(8,128)(2,1)}, u32[]{:S(2)}) copy-start(bf16[128,1408]{1,0:T(8,128)(2,1)} %param.9) | copy-start | bytes 1081348
  310.6 62.3 %all-to-all-start.5 = ((bf16[8,128,64]{1,2,0:T(8,128)(2,1)}), bf16[8,128,64]{1,2,0:T(8,128)(2,1)S(1)}, u32[]{:S(2)}, u32[]{:S(2)}) async-start(bf16[8,128,64]{1,2,0:T(8,128)(2,1)} %broadcast_in_dim.15), calls=%async_computation.5 | async-start | bytes 262144 | tf_op jit(solution)/shard_map/all_to_all | solution.py:46
Sparse Core Ops, SparseCore 0:
  19.7 74.0 all-gather.6
  310.0 61.3 all-gather.8
where the time goes:
time: 384 us; the launch traced here: 383 us
  blocking collectives  212 us (55%)
  waiting for transfers between devices  129 us (34%)
  between operations  14.9 us (4%)
  local copies, waits for them, and re-layouts  11.6 us (3%)
  other arithmetic  6.11 us (2%)
  starting transfers between devices  5.46 us (1%)
    all_gather x2, waiting for transfers between devices, stacked_from(): pieces = lax.all_gather(pieces, axes[k])  129 us
    all_to_all x3, blocking collectives, sent_to_all(): return lax.all_to_all(copies, axis, split_axis=0, concat_axis=0, tiled=True)  87.7 us
    all_to_all x1, blocking collectives, sum_at_owner(): lax.all_to_all(pieces, axis, split_axis=0, concat_axis=0, tiled=True)  81.2 us
    all_gather x2, blocking collectives, stacked_from(): pieces = lax.all_gather(pieces, axes[k])  24.3 us
    all_to_all x1, blocking collectives, on_device(): lax.all_to_all(columns, TENSOR, split_axis=0, concat_axis=1, tiled=True)  18.6 us
  transfers between devices with their start and end apart: 3, of which 2 were waited for; matrix products, arithmetic and copies ran while one was open for 1% of the time, Pallas kernels for 0%

commit v1 on v0

v1 whole, which is shorter than its diff:
```python
import math

import jax
import jax.numpy as jnp
from jax import lax
from jax.sharding import Mesh
from jax.sharding import PartitionSpec as P

FW = 11264
R = 512
AXES = ("y", "zr", "zl", "x", "c")
DP = ("y", "zr", "zl")
TENSOR = ("x", "c")
NEAR = ("y", "zl")
BF = jnp.bfloat16
F32 = jnp.float32


beta_one = 0.9
beta_two = 0.999
adam_eps = 1e-08
corr_one = 1.0 - 0.9**10
corr_two = 1.0 - 0.999**10
step_size = 0.002
decay_keep = 0.99


def exchange(x, axes):
    return lax.all_to_all(x, axes, split_axis=0, concat_axis=0, tiled=True)


def to_all(x, axes):
    n = math.prod(lax.axis_size(a) for a in axes)
    return exchange(jnp.broadcast_to(x, (n, *x.shape)), axes)


def flip_pairs():
    pairs = []
    for y in range(4):
        for z in range(16):
            for x in range(4):
                for c in range(2):
                    pairs.append((((y * 16 + z) * 4 + x) * 2 + c, ((x * 16 + z) * 4 + y) * 2 + c))
    return pairs


def adam_update(lowrank, square, first_moment, second_moment):
    bound_norm = math.sqrt(R * FW)
    factor = jnp.minimum(1.0, bound_norm / (jnp.sqrt(square) + 1e-06))
    clipped = lowrank * factor
    first = beta_one * first_moment + (1.0 - beta_one) * clipped
    second = beta_two * second_moment + (1.0 - beta_two) * clipped * clipped
    update = (first / corr_one / (jnp.sqrt(second / corr_two) + adam_eps)).astype(BF)
    return (first, second, update)


def on_device(inputs, out_grads, basis, weight, first_moment, second_moment):
    piece = basis.T.reshape(4, 2, 8, 128).transpose(1, 0, 2, 3).reshape(64, 128)
    flipped = lax.ppermute(piece, AXES, flip_pairs())
    far = to_all(flipped, ("zr",))
    halves = far.reshape(2, 1, 4, 64, 128)
    for_all = jnp.broadcast_to(halves.transpose(1, 0, 2, 3, 4), (8, 2, 4, 64, 128)).reshape(16, 4, 64, 128)
    arrived = exchange(for_all, ("y", "zl", "c"))
    slices = arrived.reshape(4, 2, 2, 4, 2, 32, 128)
    columns = slices.transpose(0, 4, 2, 5, 3, 1, 6).reshape(512, 1024)
    partial_value = lax.dot_general(
        inputs, columns, (((1,), (1,)), ((), ())), preferred_element_type=F32
    ).astype(BF)
    shares = exchange(partial_value.reshape(8, 72, 512), TENSOR)
    own_tokens = jnp.sum(shares.astype(F32), axis=0).astype(BF)
    wide = jnp.concatenate([piece[16 * k : 16 * k + 16] for k in range(4)], axis=1)
    both = to_all(jnp.concatenate([own_tokens, wide], axis=0), TENSOR)
    projected = both[:, :72].reshape(576, 512)
    back = both[:, 72:].reshape(8, 16, 4, 128).transpose(0, 2, 1, 3)
    back = back.reshape(4, 2, 2, 32, 128).transpose(0, 2, 1, 3, 4).reshape(512, 128)
    partial_low = lax.dot_general(
        projected, out_grads, (((0,), (0,)), ((), ())), preferred_element_type=F32
    ).astype(BF)
    near = exchange(partial_low.reshape(8, 64, 1408), NEAR)
    near_sum = jnp.sum(near.astype(F32), axis=0).astype(BF)
    own = exchange(near_sum.reshape(8, 8, 1408), ("zr",))
    own_rows = jnp.sum(own.astype(F32), axis=0)
    square = jnp.sum(own_rows * own_rows).reshape(1, 1)
    square = jnp.sum(to_all(square, ("y", "x", "c")), axis=0)
    square = jnp.sum(to_all(square, ("zr", "zl")), axis=0)
    first, second, update = adam_update(own_rows, square[0, 0], first_moment, second_moment)
    far_update = to_all(update, ("zr",)).reshape(64, 1408)
    all_update = to_all(far_update, NEAR).reshape(512, 1408)
    delta = lax.dot_general(back, all_update, (((0,), (0,)), ((), ())), preferred_element_type=F32)
    new_weight = (decay_keep * weight.astype(F32) - step_size * delta).astype(BF)
    return (new_weight, first, second)


def solution(mesh):
    torus = Mesh(mesh.devices.reshape(4, 8, 2, 4, 2), AXES)
    spec = P(DP, TENSOR)
    return jax.shard_map(
        on_device,
        mesh=torus,
        in_specs=(spec,) * 6,
        out_specs=(spec,) * 3,
        check_vma=False,
    )
```

time: 384 us -> 215 us (0.56)
  waiting for transfers between devices: 129 us -> 30.1 us
  blocking collectives: 212 us -> 151 us
  between operations: 14.9 us -> 1.52 us
  starting transfers between devices: 5.46 us -> 14.1 us
  local copies, waits for them, and re-layouts: 11.6 us -> 7.34 us
    all_gather x2 -> x0, waiting for transfers between devices: 129 us -> none  [stacked_from(): pieces = lax.all_gather(pieces, axes[k])]
    all_to_all x5 -> x8, blocking collectives: 188 us -> 151 us  [exchange(): return lax.all_to_all(x, axes, split_axis=0, concat_axis=0, tiled=True)]
    all_to_all x1 -> x2, waiting for transfers between devices: 0.01 us -> 26 us  [exchange(): return lax.all_to_all(x, axes, split_axis=0, concat_axis=0, tiled=True)]
    all_gather x2 -> x0, blocking collectives: 24.3 us -> none  [stacked_from(): pieces = lax.all_gather(pieces, axes[k])]
    ppermute x0 -> x1, starting transfers between devices: none -> 4.83 us  [on_device(): flipped = lax.ppermute(piece, AXES, flip_pairs())]
    ppermute x0 -> x1, waiting for transfers between devices: none -> 4.11 us  [on_device(): flipped = lax.ppermute(piece, AXES, flip_pairs())]
    all_to_all x1 -> x2, starting transfers between devices: 5.38 us -> 9.27 us  [exchange(): return lax.all_to_all(x, axes, split_axis=0, concat_axis=0, tiled=True)]
  transfers between devices with their start and end apart: 3 -> 3, of which waited for: 2 -> 3; matrix products, arithmetic and copies ran while one was open for 1% -> 0% of each run, Pallas kernels for 0% -> 0%
where the time goes in v1:
time: 215 us; the launch traced here: 214 us
  blocking collectives  151 us (70%)
  waiting for transfers between devices  30.1 us (14%)
  starting transfers between devices  14.1 us (7%)
  local copies, waits for them, and re-layouts  7.34 us (3%)
  matrix products  6.75 us (3%)
  other arithmetic  2.85 us (1%)
    all_to_all x8, blocking collectives, exchange(): return lax.all_to_all(x, axes, split_axis=0, concat_axis=0, tiled=True)  151 us
    all_to_all x2, waiting for transfers between devices, exchange(): return lax.all_to_all(x, axes, split_axis=0, concat_axis=0, tiled=True)  26 us
    all_to_all x2, starting transfers between devices, exchange(): return lax.all_to_all(x, axes, split_axis=0, concat_axis=0, tiled=True)  9.27 us
    ppermute x1, starting transfers between devices, on_device(): flipped = lax.ppermute(piece, AXES, flip_pairs())  4.83 us
  transfers between devices with their start and end apart: 3, of which 3 were waited for; matrix products, arithmetic and copies ran while one was open for 0% of the time, Pallas kernels for 0%

profile of v1, /device:TPU:6, one launch (start us, length us, event | category | flops | bytes accessed | tf_op | source)
XLA Modules:
  0.0 213.9 jit_solution(7068497374523963638)
XLA Ops:
  0.6 0.0 copy-start
  0.6 0.8 copy.18
  1.5 4.8 %collective-permute-start = (bf16[64,128]{1,0:T(8,128)(2,1)S(1)}, bf16[64,128]{1,0:T(8,128)(2,1)S(1)}, u32[]{:S(2)}, u32[]{:S(2)}) collective-permute-start(bf16[64,128]{1,0:T(8,128)(2,1)S(1)} %bitcast.39), channel_id=1, source_target_pairs={{0,0},{1,1},{2,128},{3,129},{4,256},{5,257},{6,384},{7,385},{8,8},... | collective-permute-start | bytes 49160 | tf_op jit(solution)/shard_map/ppermute | solution.py:59
  6.3 4.1 %collective-permute-done = bf16[64,128]{1,0:T(8,128)(2,1)S(1)} collective-permute-done((bf16[64,128]{1,0:T(8,128)(2,1)S(1)}, bf16[64,128]{1,0:T(8,128)(2,1)S(1)}, u32[]{:S(2)}, u32[]{:S(2)}) %collective-permute-start) | collective-permute-done | bytes 16416 | tf_op jit(solution)/shard_map/ppermute | solution.py:59
  10.5 29.7 %all_to_all.50 = bf16[8,64,128]{2,1,0:T(8,128)(2,1)S(1)} all-to-all(bf16[8,64,128]{2,1,0:T(8,128)(2,1)S(1)} %broadcast_in_dim.25), channel_id=1, replica_groups=mesh['y'=4,'zr'=8,'zl'=2,'x'=4,'c'=2] {'zr'}, dimensions={0} | all-to-all | bytes 262144 | tf_op jit(solution)/shard_map/all_to_all | solution.py:29
  40.2 0.2 broadcast_in_dim.27
  40.4 19.8 %all_to_all.51 = bf16[16,4,64,128]{3,2,1,0:T(8,128)(2,1)S(1)} all-to-all(bf16[16,4,64,128]{3,2,1,0:T(8,128)(2,1)S(1)} %bitcast.29), channel_id=1, replica_groups=mesh['y'=4,'zr'=8,'zl'=2,'x'=4,'c'=2] {'y','zl','c'}, dimensions={0} | all-to-all | bytes 2097152 | tf_op jit(solution)/shard_map/all_to_all | solution.py:29
  60.2 1.1 copy.19
  61.3 1.6 reshape.59
  62.9 3.2 %convolution_convert_fusion.1 = bf16[576,512]{1,0:T(8,128)(2,1)} fusion(bf16[576,1024]{1,0:T(8,128)(2,1)} %param.6, bf16[512,1024]{1,0:T(8,128)(2,1)} %reshape.59), kind=kOutput, calls=%fused_computation.4 | convolution fusion | flops 604274688 | bytes 2818048 | tf_op jit(solution)/shard_map/dot_general | solution.py:66
  66.1 5.6 %all-to-all-start.2 = ((bf16[8,72,512]{2,1,0:T(8,128)(2,1)}), bf16[8,72,512]{2,1,0:T(8,128)(2,1)S(1)}, u32[]{:S(2)}, u32[]{:S(2)}) async-start(bf16[8,72,512]{2,1,0:T(8,128)(2,1)} %bitcast.8), calls=%async_computation.2 | async-start | bytes 1179648 | tf_op jit(solution)/shard_map/all_to_all | solution.py:29
  71.7 8.9 %all-to-all-done.2 = bf16[8,72,512]{2,1,0:T(8,128)(2,1)S(1)} async-done(((bf16[8,72,512]{2,1,0:T(8,128)(2,1)}), bf16[8,72,512]{2,1,0:T(8,128)(2,1)S(1)}, u32[]{:S(2)}, u32[]{:S(2)}) %all-to-all-start.2) | async-done | bytes 589856 | tf_op jit(solution)/shard_map/all_to_all | solution.py:29
  80.6 0.1 reduce_sum.60
  80.8 14.9 %all_to_all.52 = bf16[8,88,512]{2,1,0:T(8,128)(2,1)S(1)} all-to-all(bf16[8,88,512]{2,1,0:T(8,128)(2,1)S(1)} %broadcast_in_dim.28), channel_id=1, replica_groups=mesh['y'=4,'zr'=8,'zl'=2,'x'=4,'c'=2] {'x','c'}, dimensions={0} | all-to-all | bytes 1441792 | tf_op jit(solution)/shard_map/all_to_all | solution.py:29
  95.6 0.9 copy-done.1
  96.6 1.4 convolution_convert_fusion
  98.0 22.5 %all_to_all.53 = bf16[8,64,1408]{2,1,0:T(8,128)(2,1)S(1)} all-to-all(bf16[8,64,1408]{2,1,0:T(8,128)(2,1)S(1)} %bitcast.31), channel_id=1, replica_groups=mesh['y'=4,'zr'=8,'zl'=2,'x'=4,'c'=2] {'y','zl'}, dimensions={0} | all-to-all | bytes 2883584 | tf_op jit(solution)/shard_map/all_to_all | solution.py:29
  120.5 0.2 reduce_sum.61
  120.7 18.5 %all_to_all.54 = bf16[8,8,1408]{2,1,0:T(8,128)(2,1)S(1)} all-to-all(bf16[8,8,1408]{2,1,0:T(8,128)(2,1)S(1)} %bitcast.32), channel_id=1, replica_groups=mesh['y'=4,'zr'=8,'zl'=2,'x'=4,'c'=2] {'zr'}, dimensions={0} | all-to-all | bytes 360448 | tf_op jit(solution)/shard_map/all_to_all | solution.py:29
  139.3 0.6 multiply_reduce_fusion
  139.9 0.7 broadcast_in_dim.29
  140.5 11.8 %all_to_all.55 = f32[32,1,1]{2,1,0:T(1,128)S(1)} all-to-all(f32[32,1,1]{2,1,0:T(1,128)S(1)} %broadcast_in_dim.29), channel_id=1, replica_groups=mesh['y'=4,'zr'=8,'zl'=2,'x'=4,'c'=2] {'y','x','c'}, dimensions={0} | all-to-all | bytes 256 | tf_op jit(solution)/shard_map/all_to_all | solution.py:29
  152.3 0.6 reduce_sum.64
  153.0 0.6 broadcast_in_dim.30
  153.6 15.0 %all_to_all.56 = f32[16,1,1]{2,1,0:T(1,128)S(1)} all-to-all(f32[16,1,1]{2,1,0:T(1,128)S(1)} %broadcast_in_dim.30), channel_id=1, replica_groups=mesh['y'=4,'zr'=8,'zl'=2,'x'=4,'c'=2] {'zr','zl'}, dimensions={0} | all-to-all | bytes 128 | tf_op jit(solution)/shard_map/all_to_all | solution.py:29
  168.6 0.6 reduce_sum.65
  170.0 0.7 divide_convert_fusion
  170.7 19.0 %all_to_all.57 = bf16[8,8,1408]{2,1,0:T(8,128)(2,1)S(1)} all-to-all(bf16[8,8,1408]{2,1,0:T(8,128)(2,1)S(1)} %broadcast_in_dim.31), channel_id=1, replica_groups=mesh['y'=4,'zr'=8,'zl'=2,'x'=4,'c'=2] {'zr'}, dimensions={0} | all-to-all | bytes 360448 | tf_op jit(solution)/shard_map/all_to_all | solution.py:29
  189.7 1.2 broadcast_in_dim.32
  190.9 3.7 %all-to-all-start.9 = ((bf16[8,64,1408]{2,1,0:T(8,128)(2,1)}), bf16[8,64,1408]{2,1,0:T(8,128)(2,1)S(1)}, u32[]{:S(2)}, u32[]{:S(2)}) async-start(bf16[8,64,1408]{2,1,0:T(8,128)(2,1)} %broadcast_in_dim.32), calls=%async_computation.9 | async-start | bytes 2883584 | tf_op jit(solution)/shard_map/all_to_all | solution.py:29
  194.7 17.0 %all-to-all-done.9 = bf16[8,64,1408]{2,1,0:T(8,128)(2,1)S(1)} async-done(((bf16[8,64,1408]{2,1,0:T(8,128)(2,1)}), bf16[8,64,1408]{2,1,0:T(8,128)(2,1)S(1)}, u32[]{:S(2)}, u32[]{:S(2)}) %all-to-all-start.9) | async-done | bytes 1441824 | tf_op jit(solution)/shard_map/all_to_all | solution.py:29
  211.8 2.1 fusion.1
  (18 shorter events, 0.2 us)
Async XLA Ops:
  0.6 95.9 %copy-start = (bf16[576,1408]{1,0:T(8,128)(2,1)S(1)}, bf16[576,1408]{1,0:T(8,128)(2,1)}, u32[]{:S(2)}) copy-start(bf16[576,1408]{1,0:T(8,128)(2,1)} %param.7) | copy-start | bytes 4866052
  1.5 8.9 %collective-permute-start = (bf16[64,128]{1,0:T(8,128)(2,1)S(1)}, bf16[64,128]{1,0:T(8,128)(2,1)S(1)}, u32[]{:S(2)}, u32[]{:S(2)}) collective-permute-start(bf16[64,128]{1,0:T(8,128)(2,1)S(1)} %bitcast.39), channel_id=1, source_target_pairs={{0,0},{1,1},{2,128},{3,129},{4,256},{5,257},{6,384},{7,385},{8,8},... | collective-permute-start | bytes 49160 | tf_op jit(solution)/shard_map/ppermute | solution.py:59
  66.1 14.5 %all-to-all-start.2 = ((bf16[8,72,512]{2,1,0:T(8,128)(2,1)}), bf16[8,72,512]{2,1,0:T(8,128)(2,1)S(1)}, u32[]{:S(2)}, u32[]{:S(2)}) async-start(bf16[8,72,512]{2,1,0:T(8,128)(2,1)} %bitcast.8), calls=%async_computation.2 | async-start | bytes 1179648 | tf_op jit(solution)/shard_map/all_to_all | solution.py:29
  95.6 0.9 copy-start.1
  120.5 49.5 %copy-start.2 = (f32[8,1408]{1,0:T(8,128)S(1)}, f32[8,1408]{1,0:T(8,128)}, u32[]{:S(2)}) copy-start(f32[8,1408]{1,0:T(8,128)} %param.10) | copy-start | bytes 135172
  120.5 49.5 %copy-start.3 = (f32[8,1408]{1,0:T(8,128)S(1)}, f32[8,1408]{1,0:T(8,128)}, u32[]{:S(2)}) copy-start(f32[8,1408]{1,0:T(8,128)} %param.11) | copy-start | bytes 135172
  190.9 3.7 %slice-start = ((bf16[8,88,512]{2,1,0:T(8,128)(2,1)}), bf16[8,16,512]{2,1,0:T(8,128)(2,1)S(1)}, s32[]{:S(2)}) async-start(bf16[8,88,512]{2,1,0:T(8,128)(2,1)} %copy-done.1), calls=%async_computation.10 | async-start | bytes 262144 | tf_op jit(solution)/shard_map/slice | solution.py:74
  190.9 20.8 %all-to-all-start.9 = ((bf16[8,64,1408]{2,1,0:T(8,128)(2,1)}), bf16[8,64,1408]{2,1,0:T(8,128)(2,1)S(1)}, u32[]{:S(2)}, u32[]{:S(2)}) async-start(bf16[8,64,1408]{2,1,0:T(8,128)(2,1)} %broadcast_in_dim.32), calls=%async_computation.9 | async-start | bytes 2883584 | tf_op jit(solution)/shard_map/all_to_all | solution.py:29

commit v2 on v1

v2 whole, which is shorter than its diff:
```python
import math

import jax
import jax.numpy as jnp
from jax import lax
from jax.experimental import pallas as pl
from jax.experimental.pallas import tpu as pltpu
from jax.sharding import Mesh
from jax.sharding import PartitionSpec as P

FW = 11264
R = 512
AXES = ("y", "zr", "zl", "x", "c")
DP = ("y", "zr", "zl")
TENSOR = ("x", "c")
NEAR = ("y", "zl")
PLANE = ("y", "zl", "x", "c")
BF = jnp.bfloat16
F32 = jnp.float32


beta_one = 0.9
beta_two = 0.999
adam_eps = 1e-08
corr_one = 1.0 - 0.9**10
corr_two = 1.0 - 0.999**10
step_size = 0.002
decay_keep = 0.99


def exchange(x, axes):
    return lax.all_to_all(x, axes, split_axis=0, concat_axis=0, tiled=True)


def to_all(x, axes):
    n = math.prod(lax.axis_size(a) for a in axes)
    return exchange(jnp.broadcast_to(x, (n, *x.shape)), axes)


def shape(dims, dtype):
    return jax.ShapeDtypeStruct(dims, dtype)


def small(mib):
    return pltpu.CompilerParams(vmem_limit_bytes=mib * 2**20)


def project_kernel(inputs, blocks, out, columns):
    for y in range(4):
        for zl in range(2):
            for high in range(2):
                for mid in range(2):
                    row = 16 * (((y * 2 + zl) * 2 + high) * 2 + mid)
                    for f in range(8):
                        columns[row : row + 16, 128 * f : 128 * f + 128] = blocks[
                            zl * 2 + mid, f % 2, y, high, f // 2
                        ]
    out[...] = lax.dot_general(
        inputs[...], columns[...], (((1,), (1,)), ((), ())), preferred_element_type=F32
    ).astype(BF)


def project(inputs, blocks):
    return pl.pallas_call(
        project_kernel,
        out_shape=shape((576, 512), BF),
        scratch_shapes=[pltpu.VMEM((512, 1024), BF)],
        compiler_params=small(16),
        name="project",
    )(inputs, blocks)


def near_kernel(parts, out):
    out[...] = jnp.sum(parts[...].astype(F32), axis=0).astype(BF)


def near_sum(parts):
    return pl.pallas_call(
        near_kernel,
        out_shape=shape((64, 1408), BF),
        compiler_params=small(8),
        name="near_sum",
    )(parts)


def own_kernel(parts, rows, square):
    own = jnp.sum(parts[...].astype(F32), axis=0)
    rows[...] = own
    lanes = jnp.zeros((1, 128), F32)
    squares = own * own
    for k in range(11):
        lanes += jnp.sum(squares[:, 128 * k : 128 * k + 128], axis=0, keepdims=True)
    square[...] = jnp.broadcast_to(lanes[None], (64, 1, 128))


def own_sum(parts):
    return pl.pallas_call(
        own_kernel,
        out_shape=(shape((8, 1408), F32), shape((64, 1, 128), F32)),
        compiler_params=small(4),
        name="own_sum",
    )(parts)


def plane_kernel(parts, out):
    total = jnp.sum(parts[...], axis=0, keepdims=True)
    out[...] = jnp.broadcast_to(total, (8, 1, 128))


def plane_sum(parts):
    return pl.pallas_call(
        plane_kernel,
        out_shape=shape((8, 1, 128), F32),
        compiler_params=small(2),
        name="plane_sum",
    )(parts)


def adam_kernel(lowrank, square, first_moment, second_moment, new_first, new_second, update):
    bound_norm = math.sqrt(R * FW)
    total = jnp.sum(jnp.sum(square[...], axis=0), axis=1, keepdims=True)
    factor = jnp.minimum(1.0, bound_norm / (jnp.sqrt(total) + 1e-06))
    clipped = lowrank[...] * factor
    first = beta_one * first_moment[...] + (1.0 - beta_one) * clipped
    second = beta_two * second_moment[...] + (1.0 - beta_two) * clipped * clipped
    new_first[...] = first
    new_second[...] = second
    step = (first / corr_one / (jnp.sqrt(second / corr_two) + adam_eps)).astype(BF)
    for k in range(8):
        update[k] = step


def adam(lowrank, square, first_moment, second_moment):
    return pl.pallas_call(
        adam_kernel,
        out_shape=(shape((8, 1408), F32), shape((8, 1408), F32), shape((8, 8, 1408), BF)),
        compiler_params=small(4),
        name="adam",
    )(lowrank, square, first_moment, second_moment)


def apply_kernel(both, update, weight, out, back):
    for y in range(4):
        for high in range(2):
            for k in range(4):
                row = ((y * 2 + k // 2) * 2 + high) * 32 + (k % 2) * 16
                back[row : row + 16, :] = both[y * 2 + high, :16, 128 * k : 128 * k + 128]
    delta = lax.dot_general(
        back[...], update[...], (((0,), (0,)), ((), ())), preferred_element_type=F32
    )
    out[...] = (decay_keep * weight[...].astype(F32) - step_size * delta).astype(BF)


def apply_update(both, update, weight):
    return pl.pallas_call(
        apply_kernel,
        out_shape=shape((128, 1408), BF),
        scratch_shapes=[pltpu.VMEM((512, 128), BF)],
        compiler_params=small(12),
        name="apply_update",
    )(both, update, weight)


def on_device(inputs, out_grads, basis, weight, first_moment, second_moment):
    piece = basis.T.reshape(4, 2, 8, 128).transpose(1, 0, 2, 3).reshape(64, 128)
    quarters = jnp.broadcast_to(piece.reshape(4, 1, 16, 128), (4, 8, 16, 128))
    wide = jnp.concatenate([piece[16 * k : 16 * k + 16] for k in range(4)], axis=1)
    quarters, wide = lax.optimization_barrier((quarters, wide))
    far = exchange(quarters.reshape(32, 16, 128), ("y", "zr"))
    copies = jnp.broadcast_to(far.reshape(1, 8, 4, 16, 128), (8, 8, 4, 16, 128))
    slices = exchange(copies.reshape(64, 4, 16, 128), PLANE)
    partial_value = project(inputs, slices.reshape(4, 2, 4, 2, 4, 16, 128))
    shares = exchange(partial_value.reshape(8, 72, 512), TENSOR)
    own_tokens = jnp.sum(shares.astype(F32), axis=0).astype(BF)
    both = to_all(jnp.concatenate([wide, own_tokens], axis=0), TENSOR)
    projected = both[:, 16:].reshape(576, 512)
    partial_low = lax.dot_general(
        projected, out_grads, (((0,), (0,)), ((), ())), preferred_element_type=F32
    ).astype(BF)
    near = exchange(partial_low.reshape(8, 64, 1408), NEAR)
    own = exchange(near_sum(near).reshape(8, 8, 1408), ("zr",))
    own_rows, square = own_sum(own)
    square = plane_sum(exchange(square, PLANE))
    first, second, update = adam(own_rows, exchange(square, ("zr",)), first_moment, second_moment)
    far_update = exchange(update, ("zr",)).reshape(64, 1408)
    all_update = to_all(far_update, NEAR).reshape(512, 1408)
    new_weight = apply_update(both, all_update, weight)
    return (new_weight, first, second)


def solution(mesh):
    torus = Mesh(mesh.devices.reshape(4, 8, 2, 4, 2), AXES)
    spec = P(DP, TENSOR)
    return jax.shard_map(
        on_device,
        mesh=torus,
        in_specs=(spec,) * 6,
        out_specs=(spec,) * 3,
        check_vma=False,
    )
```

time: 215 us -> 202 us (0.940)
  blocking collectives: 151 us -> 195 us
  waiting for transfers between devices: 30.1 us -> 0 us
  starting transfers between devices: 14.1 us -> 0 us
  local copies, waits for them, and re-layouts: 7.34 us -> 1.33 us
  matrix products: 6.75 us -> 1.41 us
  Pallas kernels: 0 us -> 3.1 us
  other arithmetic: 2.85 us -> 0.1 us
    all_to_all x8 -> x10, blocking collectives: 151 us -> 195 us  [exchange(): return lax.all_to_all(x, axes, split_axis=0, concat_axis=0, tiled=True)]
    all_to_all x2 -> x0, waiting for transfers between devices: 26 us -> none  [exchange(): return lax.all_to_all(x, axes, split_axis=0, concat_axis=0, tiled=True)]
    all_to_all x2 -> x0, starting transfers between devices: 9.27 us -> none  [exchange(): return lax.all_to_all(x, axes, split_axis=0, concat_axis=0, tiled=True)]
    dot_general x2 -> x0, matrix products: 5.34 us -> none  [the longest x1 3.22 us: on_device(): lax.dot_general(inputs, columns, (((1,), (1,)), ((), ())), preferred_elem...]
    ppermute x1 -> x0, starting transfers between devices: 4.83 us -> none  [on_device(): flipped = lax.ppermute(piece, AXES, flip_pairs())]
    ppermute x1 -> x0, waiting for transfers between devices: 4.11 us -> none  [on_device(): flipped = lax.ppermute(piece, AXES, flip_pairs())]
    pallas_call x0 -> x6, Pallas kernels: none -> 3.1 us  [the longest x1 1.16 us: apply_update(): pl.pallas_call(apply_kernel, out_shape=shape((128, 1408), BF), scratch_sh...]
    broadcast_in_dim x6 -> x2, local copies, waits for them, and re-layouts: 2.61 us -> 0.16 us  [to_all(): return exchange(jnp.broadcast_to(x, (n, *x.shape)), axes)]
  transfers between devices with their start and end apart: 3 -> 0, of which waited for: 3 -> 0; matrix products, arithmetic and copies ran while one was open for 0% -> 0% of each run, Pallas kernels for 0% -> 0%
where the time goes in v2:
time: 202 us; the launch traced here: 201 us
  blocking collectives  195 us (97%)
  Pallas kernels  3.1 us (2%)
    all_to_all x10, blocking collectives, exchange(): return lax.all_to_all(x, axes, split_axis=0, concat_axis=0, tiled=True)  195 us

profile of v2, /device:TPU:6, one launch (start us, length us, event | category | flops | bytes accessed | tf_op | source)
XLA Modules:
  0.0 201.4 jit_solution(6873012685836666454)
XLA Ops:
  0.6 0.0 copy-start
  0.6 0.8 copy.11
  1.5 34.5 %all_to_all.50 = bf16[32,16,128]{2,1,0:T(8,128)(2,1)S(1)} all-to-all(bf16[32,16,128]{2,1,0:T(8,128)(2,1)S(1)} %bitcast.28), channel_id=1, replica_groups=mesh['y'=4,'zr'=8,'zl'=2,'x'=4,'c'=2] {'y','zr'}, dimensions={0} | all-to-all | bytes 262144 | tf_op jit(solution)/shard_map/all_to_all | solution.py:32
  36.0 0.0 copy-start.1
  36.0 0.2 broadcast_in_dim.23
  36.3 21.9 %all_to_all.51 = bf16[64,4,16,128]{3,2,1,0:T(8,128)(2,1)S(1)} all-to-all(bf16[64,4,16,128]{3,2,1,0:T(8,128)(2,1)S(1)} %bitcast.23), channel_id=1, replica_groups=mesh['y'=4,'zr'=8,'zl'=2,'x'=4,'c'=2] {'y','zl','x','c'}, dimensions={0} | all-to-all | bytes 2097152 | tf_op jit(solution)/shard_map/all_to_all | solution.py:32
  58.2 0.0 copy-done.1
  58.2 0.9 project.1
  59.1 14.6 %all_to_all.52 = bf16[8,72,512]{2,1,0:T(8,128)(2,1)S(1)} all-to-all(bf16[8,72,512]{2,1,0:T(8,128)(2,1)S(1)} %bitcast.21), channel_id=1, replica_groups=mesh['y'=4,'zr'=8,'zl'=2,'x'=4,'c'=2] {'x','c'}, dimensions={0} | all-to-all | bytes 1179648 | tf_op jit(solution)/shard_map/all_to_all | solution.py:32
  73.6 0.1 reduce_sum.12
  73.8 14.9 %all_to_all.53.both = bf16[8,88,512]{2,1,0:T(8,128)(2,1)S(1)} all-to-all(bf16[8,88,512]{2,1,0:T(8,128)(2,1)S(1)} %broadcast_in_dim.24), channel_id=1, replica_groups=mesh['y'=4,'zr'=8,'zl'=2,'x'=4,'c'=2] {'x','c'}, dimensions={0} | all-to-all | bytes 1441792 | tf_op jit(solution)/shard_map/all_to_all | solution.py:32
  88.7 0.0 copy-done
  88.7 1.4 convolution_convert_fusion
  90.1 22.6 %all_to_all.54.parts = bf16[8,64,1408]{2,1,0:T(8,128)(2,1)S(1)} all-to-all(bf16[8,64,1408]{2,1,0:T(8,128)(2,1)S(1)} %bitcast.24), channel_id=1, replica_groups=mesh['y'=4,'zr'=8,'zl'=2,'x'=4,'c'=2] {'y','zl'}, dimensions={0} | all-to-all | bytes 2883584 | tf_op jit(solution)/shard_map/all_to_all | solution.py:32
  112.8 0.0 copy-start.3
  112.8 0.0 copy-start.4
  112.8 0.2 near_sum.1
  112.9 18.6 %all_to_all.55.parts = bf16[8,8,1408]{2,1,0:T(8,128)(2,1)S(1)} all-to-all(bf16[8,8,1408]{2,1,0:T(8,128)(2,1)S(1)} %bitcast.22), channel_id=1, replica_groups=mesh['y'=4,'zr'=8,'zl'=2,'x'=4,'c'=2] {'zr'}, dimensions={0} | all-to-all | bytes 360448 | tf_op jit(solution)/shard_map/all_to_all | solution.py:32
  131.5 0.1 own_sum.1
  131.6 13.1 %all_to_all.56.parts = f32[64,1,128]{2,1,0:T(1,128)S(1)} all-to-all(f32[64,1,128]{2,1,0:T(1,128)S(1)} %get-tuple-element.13), channel_id=1, replica_groups=mesh['y'=4,'zr'=8,'zl'=2,'x'=4,'c'=2] {'y','zl','x','c'}, dimensions={0} | all-to-all | bytes 65536 | tf_op jit(solution)/shard_map/all_to_all | solution.py:32
  144.7 0.1 plane_sum.1
  144.7 15.3 %all_to_all.57.square = f32[8,1,128]{2,1,0:T(1,128)S(1)} all-to-all(f32[8,1,128]{2,1,0:T(1,128)S(1)} %plane_sum.1), channel_id=1, replica_groups=mesh['y'=4,'zr'=8,'zl'=2,'x'=4,'c'=2] {'zr'}, dimensions={0} | all-to-all | bytes 8192 | tf_op jit(solution)/shard_map/all_to_all | solution.py:32
  160.1 0.0 copy-done.3
  160.1 0.0 copy-done.4
  160.1 0.7 adam.1
  160.8 18.7 %all_to_all.58 = bf16[8,8,1408]{2,1,0:T(8,128)(2,1)S(1)} all-to-all(bf16[8,8,1408]{2,1,0:T(8,128)(2,1)S(1)} %get-tuple-element.14), channel_id=1, replica_groups=mesh['y'=4,'zr'=8,'zl'=2,'x'=4,'c'=2] {'zr'}, dimensions={0} | all-to-all | bytes 360448 | tf_op jit(solution)/shard_map/all_to_all | solution.py:32
  179.5 0.1 broadcast_in_dim.25
  179.6 0.0 copy-start.2
  179.6 20.6 %all_to_all.59 = bf16[8,64,1408]{2,1,0:T(8,128)(2,1)S(1)} all-to-all(bf16[8,64,1408]{2,1,0:T(8,128)(2,1)S(1)} %broadcast_in_dim.25), channel_id=1, replica_groups=mesh['y'=4,'zr'=8,'zl'=2,'x'=4,'c'=2] {'y','zl'}, dimensions={0} | all-to-all | bytes 2883584 | tf_op jit(solution)/shard_map/all_to_all | solution.py:32
  200.2 0.0 copy-done.2
  200.2 1.2 apply_update.1
  (6 shorter events, 0.1 us)
Async XLA Ops:
  0.6 88.1 %copy-start = (bf16[576,1408]{1,0:T(8,128)(2,1)S(1)}, bf16[576,1408]{1,0:T(8,128)(2,1)}, u32[]{:S(2)}) copy-start(bf16[576,1408]{1,0:T(8,128)(2,1)} %param.7) | copy-start | bytes 4866052
  36.0 22.2 %copy-start.1 = (bf16[576,1024]{1,0:T(8,128)(2,1)S(1)}, bf16[576,1024]{1,0:T(8,128)(2,1)}, u32[]{:S(2)}) copy-start(bf16[576,1024]{1,0:T(8,128)(2,1)} %inputs.1) | copy-start | bytes 3538948
  112.8 47.3 %copy-start.3 = (f32[8,1408]{1,0:T(8,128)S(1)}, f32[8,1408]{1,0:T(8,128)}, u32[]{:S(2)}) copy-start(f32[8,1408]{1,0:T(8,128)} %first_moment.1) | copy-start | bytes 135172
  112.8 47.3 %copy-start.4 = (f32[8,1408]{1,0:T(8,128)S(1)}, f32[8,1408]{1,0:T(8,128)}, u32[]{:S(2)}) copy-start(f32[8,1408]{1,0:T(8,128)} %second_moment.1) | copy-start | bytes 135172
  179.6 20.6 %copy-start.2 = (bf16[128,1408]{1,0:T(8,128)(2,1)S(1)}, bf16[128,1408]{1,0:T(8,128)(2,1)}, u32[]{:S(2)}) copy-start(bf16[128,1408]{1,0:T(8,128)(2,1)} %weight.1) | copy-start | bytes 1081348

commit v3 on v2

--- a/solution.py
+++ b/solution.py
@@ -7,6 +7,7 @@
 from jax.experimental.pallas import tpu as pltpu
 from jax.sharding import Mesh
 from jax.sharding import PartitionSpec as P
+
 
 FW = 11264
 R = 512
@@ -45,29 +46,50 @@
     return pltpu.CompilerParams(vmem_limit_bytes=mib * 2**20)
 
 
-def project_kernel(inputs, blocks, out, columns):
-    for y in range(4):
-        for zl in range(2):
+def project_kernel(inputs, blocks, wide, out, columns):
+    for zl in range(2):
+        for y in range(4):
             for high in range(2):
                 for mid in range(2):
-                    row = 16 * (((y * 2 + zl) * 2 + high) * 2 + mid)
+                    row = 16 * (((zl * 4 + y) * 2 + high) * 2 + mid)
                     for f in range(8):
                         columns[row : row + 16, 128 * f : 128 * f + 128] = blocks[
                             zl * 2 + mid, f % 2, y, high, f // 2
                         ]
-    out[...] = lax.dot_general(
+    partial_value = lax.dot_general(
         inputs[...], columns[...], (((1,), (1,)), ((), ())), preferred_element_type=F32
-    ).astype(BF)
-
-
-def project(inputs, blocks):
+    )
+    for t in range(8):
+        out[t, :16] = wide[...]
+        out[t, 16:] = partial_value[72 * t : 72 * t + 72].astype(BF)
+
+
+def project(inputs, blocks, wide):
     return pl.pallas_call(
         project_kernel,
-        out_shape=shape((576, 512), BF),
+        out_shape=shape((8, 88, 512), BF),
         scratch_shapes=[pltpu.VMEM((512, 1024), BF)],
         compiler_params=small(16),
         name="project",
-    )(inputs, blocks)
+    )(inputs, blocks, wide)
+
+
+def lowrank_kernel(parity, tokens, own_grads, pair_grads, out):
+    contract = (((0,), (0,)), ((), ()))
+    own = lax.dot_general(tokens[parity[0]], own_grads[...], contract, preferred_element_type=F32)
+    pair = lax.dot_general(tokens[1 - parity[0]], pair_grads[...], contract, preferred_element_type=F32)
+    out[...] = (own + pair).astype(BF)
+
+
+def pair_lowrank(parity, tokens, own_grads, pair_grads):
+    whole = pl.BlockSpec(memory_space=pltpu.VMEM)
+    return pl.pallas_call(
+        lowrank_kernel,
+        in_specs=[pl.BlockSpec(memory_space=pltpu.SMEM), whole, whole, whole],
+        out_shape=shape((256, 1408), BF),
+        compiler_params=small(16),
+        name="pair_lowrank",
+    )(parity, tokens, own_grads, pair_grads)
 
 
 def near_kernel(parts, out):
@@ -161,30 +183,31 @@
     )(both, update, weight)
 
 
-def on_device(inputs, out_grads, basis, weight, first_moment, second_moment):
+def body(inputs, out_grads, basis, weight, first_moment, second_moment):
+    pair_grads = lax.ppermute(out_grads, "zl", [(0, 1), (1, 0)])
+    parity = lax.axis_index("zl").reshape(1)
     piece = basis.T.reshape(4, 2, 8, 128).transpose(1, 0, 2, 3).reshape(64, 128)
     quarters = jnp.broadcast_to(piece.reshape(4, 1, 16, 128), (4, 8, 16, 128))
     wide = jnp.concatenate([piece[16 * k : 16 * k + 16] for k in range(4)], axis=1)
-    quarters, wide = lax.optimization_barrier((quarters, wide))
+    quarters, wide, parity = lax.optimization_barrier((quarters, wide, parity))
     far = exchange(quarters.reshape(32, 16, 128), ("y", "zr"))
     copies = jnp.broadcast_to(far.reshape(1, 8, 4, 16, 128), (8, 8, 4, 16, 128))
     slices = exchange(copies.reshape(64, 4, 16, 128), PLANE)
-    partial_value = project(inputs, slices.reshape(4, 2, 4, 2, 4, 16, 128))
-    shares = exchange(partial_value.reshape(8, 72, 512), TENSOR)
-    own_tokens = jnp.sum(shares.astype(F32), axis=0).astype(BF)
-    both = to_all(jnp.concatenate([wide, own_tokens], axis=0), TENSOR)
-    projected = both[:, 16:].reshape(576, 512)
-    partial_low = lax.dot_general(
-        projected, out_grads, (((0,), (0,)), ((), ())), preferred_element_type=F32
-    ).astype(BF)
-    near = exchange(partial_low.reshape(8, 64, 1408), NEAR)
+    partial_value = project(inputs, slices.reshape(4, 2, 4, 2, 4, 16, 128), wide)
+    partial_value, pair_grads = lax.optimization_barrier((partial_value, pair_grads))
+    shares = exchange(partial_value, TENSOR)
+    own_tokens = jnp.sum(shares[:, 16:].astype(F32), axis=0).astype(BF)
+    halves = [jnp.broadcast_to(own_tokens[:, 256 * k : 256 * k + 256], (8, 72, 256)) for k in range(2)]
+    tokens = exchange(jnp.concatenate(halves), ("zl", "x", "c")).reshape(2, 576, 256)
+    partial_low = pair_lowrank(parity, tokens, out_grads, pair_grads)
+    near = exchange(partial_low.reshape(4, 64, 1408), ("y",))
     own = exchange(near_sum(near).reshape(8, 8, 1408), ("zr",))
     own_rows, square = own_sum(own)
     square = plane_sum(exchange(square, PLANE))
     first, second, update = adam(own_rows, exchange(square, ("zr",)), first_moment, second_moment)
     far_update = exchange(update, ("zr",)).reshape(64, 1408)
     all_update = to_all(far_update, NEAR).reshape(512, 1408)
-    new_weight = apply_update(both, all_update, weight)
+    new_weight = apply_update(shares, all_update, weight)
     return (new_weight, first, second)
 
 
@@ -192,7 +215,7 @@
     torus = Mesh(mesh.devices.reshape(4, 8, 2, 4, 2), AXES)
     spec = P(DP, TENSOR)
     return jax.shard_map(
-        on_device,
+        body,
         mesh=torus,
         in_specs=(spec,) * 6,
         out_specs=(spec,) * 3,

time: 202 us -> 230 us (1.14)
  waiting for transfers between devices: 0 us -> 42.8 us
  blocking collectives: 195 us -> 166 us
  starting transfers between devices: 0 us -> 10.2 us
  Pallas kernels: 3.1 us -> 5.81 us
    ppermute x0 -> x1, waiting for transfers between devices: none -> 30.6 us  [body(): pair_grads = lax.ppermute(out_grads, 'zl', [(0, 1), (1, 0)])]
    all_to_all x10 -> x9, blocking collectives: 195 us -> 166 us  [exchange(): return lax.all_to_all(x, axes, split_axis=0, concat_axis=0, tiled=True)]
    all_to_all x0 -> x1, waiting for transfers between devices: none -> 12.2 us  [exchange(): return lax.all_to_all(x, axes, split_axis=0, concat_axis=0, tiled=True)]
    all_to_all x0 -> x1, starting transfers between devices: none -> 6.8 us  [exchange(): return lax.all_to_all(x, axes, split_axis=0, concat_axis=0, tiled=True)]
    ppermute x0 -> x1, starting transfers between devices: none -> 3.38 us  [body(): pair_grads = lax.ppermute(out_grads, 'zl', [(0, 1), (1, 0)])]
    pallas_call x1 -> x2, Pallas kernels: 0.88 us -> 3.68 us  [the longest x1 2.81 us: pair_lowrank(): pl.pallas_call(lowrank_kernel, in_specs=[pl.BlockSpec(memory_space=pltpu....]
  transfers between devices with their start and end apart: 0 -> 2, of which waited for: 0 -> 2; matrix products, arithmetic and copies ran while one was open for 0% -> 0% of each run, Pallas kernels for 0% -> 0%
where the time goes in v3:
time: 230 us
  blocking collectives  166 us (72%)
  waiting for transfers between devices  42.8 us (19%)
  starting transfers between devices  10.2 us (4%)
  Pallas kernels  5.81 us (3%)
  local copies, waits for them, and re-layouts  3.44 us (1%)
    all_to_all x9, blocking collectives, exchange(): return lax.all_to_all(x, axes, split_axis=0, concat_axis=0, tiled=True)  166 us
    ppermute x1, waiting for transfers between devices, body(): pair_grads = lax.ppermute(out_grads, 'zl', [(0, 1), (1, 0)])  30.6 us
    all_to_all x1, waiting for transfers between devices, exchange(): return lax.all_to_all(x, axes, split_axis=0, concat_axis=0, tiled=True)  12.2 us
    all_to_all x1, starting transfers between devices, exchange(): return lax.all_to_all(x, axes, split_axis=0, concat_axis=0, tiled=True)  6.8 us
  transfers between devices with their start and end apart: 2, of which 2 were waited for; matrix products, arithmetic and copies ran while one was open for 0% of the time, Pallas kernels for 0%

profile of v3, /device:TPU:6, one launch (start us, length us, event | category | flops | bytes accessed | tf_op | source)
XLA Modules:
  0.0 229.5 jit_solution(16305129814920833967)
XLA Ops:
  0.6 0.7 copy.9
  1.4 34.5 %all_to_all.50 = bf16[32,16,128]{2,1,0:T(8,128)(2,1)S(1)} all-to-all(bf16[32,16,128]{2,1,0:T(8,128)(2,1)S(1)} %bitcast.26), channel_id=1, replica_groups=mesh['y'=4,'zr'=8,'zl'=2,'x'=4,'c'=2] {'y','zr'}, dimensions={0} | all-to-all | bytes 262144 | tf_op jit(solution)/shard_map/all_to_all | solution.py:33
  35.9 1.2 broadcast_in_dim.26
  37.1 6.8 %all-to-all-start.1 = ((bf16[64,4,16,128]{3,2,1,0:T(8,128)(2,1)}), bf16[64,4,16,128]{3,2,1,0:T(8,128)(2,1)S(1)}, u32[]{:S(2)}, u32[]{:S(2)}) async-start(bf16[64,4,16,128]{3,2,1,0:T(8,128)(2,1)} %bitcast.23), calls=%async_computation.1 | async-start | bytes 2097152 | tf_op jit(solution)/shard_map/all_to_all | solution.py:33
  43.9 0.0 copy-done
  43.9 3.4 %collective-permute-start = (bf16[576,1408]{1,0:T(8,128)(2,1)S(1)}, bf16[576,1408]{1,0:T(8,128)(2,1)}, u32[]{:S(2)}, u32[]{:S(2)}) collective-permute-start(bf16[576,1408]{1,0:T(8,128)(2,1)S(1)} %copy-done), channel_id=1, source_target_pairs={{0,8},{8,0},{1,9},{9,1},{2,10},{10,2},{3,11},{11,3},{4,12},{12,4},... | collective-permute-start | bytes 4866056 | tf_op jit(solution)/shard_map/ppermute | solution.py:187
  47.3 12.2 %all-to-all-done.1 = bf16[64,4,16,128]{3,2,1,0:T(8,128)(2,1)S(1)} async-done(((bf16[64,4,16,128]{3,2,1,0:T(8,128)(2,1)}), bf16[64,4,16,128]{3,2,1,0:T(8,128)(2,1)S(1)}, u32[]{:S(2)}, u32[]{:S(2)}) %all-to-all-start.1) | async-done | bytes 1048608 | tf_op jit(solution)/shard_map/all_to_all | solution.py:33
  59.5 1.3 copy-done.1
  60.8 0.9 project.1
  61.7 30.6 %collective-permute-done.pair_grads = bf16[576,1408]{1,0:T(8,128)(2,1)} collective-permute-done((bf16[576,1408]{1,0:T(8,128)(2,1)S(1)}, bf16[576,1408]{1,0:T(8,128)(2,1)}, u32[]{:S(2)}, u32[]{:S(2)}) %collective-permute-start) | collective-permute-done | bytes 1622048 | tf_op jit(solution)/shard_map/ppermute | solution.py:187
  92.3 15.0 %all_to_all.51.both = bf16[8,88,512]{2,1,0:T(8,128)(2,1)S(1)} all-to-all(bf16[8,88,512]{2,1,0:T(8,128)(2,1)S(1)} %project.1), channel_id=1, replica_groups=mesh['y'=4,'zr'=8,'zl'=2,'x'=4,'c'=2] {'x','c'}, dimensions={0} | all-to-all | bytes 1441792 | tf_op jit(solution)/shard_map/all_to_all | solution.py:33
  107.3 0.1 slice_reduce_fusion
  107.4 0.1 pad_maximum_fusion
  107.5 14.2 %all_to_all.52 = bf16[16,72,256]{2,1,0:T(8,128)(2,1)S(1)} all-to-all(bf16[16,72,256]{2,1,0:T(8,128)(2,1)S(1)} %pad_maximum_fusion), channel_id=1, replica_groups=mesh['y'=4,'zr'=8,'zl'=2,'x'=4,'c'=2] {'zl','x','c'}, dimensions={0} | all-to-all | bytes 1179648 | tf_op jit(solution)/shard_map/all_to_all | solution.py:33
  121.7 2.8 %pair_lowrank.1 = bf16[256,1408]{1,0:T(8,128)(2,1)S(1)} custom-call(s32[1]{0:T(128)} %bitcast.6.parity, bf16[2,576,256]{2,1,0:T(8,128)(2,1)S(1)} %bitcast.21, bf16[576,1408]{1,0:T(8,128)(2,1)S(1)} %copy-done, bf16[576,1408]{1,0:T(8,128)(2,1)} %collective-permute-done.pair_grads), custom_call_target="tpu_custom_call" | custom-call | tf_op jit(solution)/shard_map/pair_lowrank/pallas_call | solution.py:86
  124.5 0.0 copy-start.3
  124.6 0.0 copy-start.4
  124.6 16.2 %all_to_all.53.parts = bf16[4,64,1408]{2,1,0:T(8,128)(2,1)S(1)} all-to-all(bf16[4,64,1408]{2,1,0:T(8,128)(2,1)S(1)} %bitcast.20), channel_id=1, replica_groups=mesh['y'=4,'zr'=8,'zl'=2,'x'=4,'c'=2] {'y'}, dimensions={0} | all-to-all | bytes 1441792 | tf_op jit(solution)/shard_map/all_to_all | solution.py:33
  140.8 0.1 near_sum.1
  140.9 19.7 %all_to_all.54.parts = bf16[8,8,1408]{2,1,0:T(8,128)(2,1)S(1)} all-to-all(bf16[8,8,1408]{2,1,0:T(8,128)(2,1)S(1)} %bitcast.22), channel_id=1, replica_groups=mesh['y'=4,'zr'=8,'zl'=2,'x'=4,'c'=2] {'zr'}, dimensions={0} | all-to-all | bytes 360448 | tf_op jit(solution)/shard_map/all_to_all | solution.py:33
  160.6 0.1 own_sum.1
  160.6 12.1 %all_to_all.55.parts = f32[64,1,128]{2,1,0:T(1,128)S(1)} all-to-all(f32[64,1,128]{2,1,0:T(1,128)S(1)} %get-tuple-element.19), channel_id=1, replica_groups=mesh['y'=4,'zr'=8,'zl'=2,'x'=4,'c'=2] {'y','zl','x','c'}, dimensions={0} | all-to-all | bytes 65536 | tf_op jit(solution)/shard_map/all_to_all | solution.py:33
  172.8 0.1 plane_sum.1
  172.9 15.4 %all_to_all.56.square = f32[8,1,128]{2,1,0:T(1,128)S(1)} all-to-all(f32[8,1,128]{2,1,0:T(1,128)S(1)} %plane_sum.1), channel_id=1, replica_groups=mesh['y'=4,'zr'=8,'zl'=2,'x'=4,'c'=2] {'zr'}, dimensions={0} | all-to-all | bytes 8192 | tf_op jit(solution)/shard_map/all_to_all | solution.py:33
  188.2 0.0 copy-done.3
  188.2 0.7 adam.1
  189.0 18.7 %all_to_all.57 = bf16[8,8,1408]{2,1,0:T(8,128)(2,1)S(1)} all-to-all(bf16[8,8,1408]{2,1,0:T(8,128)(2,1)S(1)} %get-tuple-element.20), channel_id=1, replica_groups=mesh['y'=4,'zr'=8,'zl'=2,'x'=4,'c'=2] {'zr'}, dimensions={0} | all-to-all | bytes 360448 | tf_op jit(solution)/shard_map/all_to_all | solution.py:33
  207.6 0.1 broadcast_in_dim.29
  207.7 0.0 copy-start.2
  207.7 20.6 %all_to_all.58 = bf16[8,64,1408]{2,1,0:T(8,128)(2,1)S(1)} all-to-all(bf16[8,64,1408]{2,1,0:T(8,128)(2,1)S(1)} %broadcast_in_dim.29), channel_id=1, replica_groups=mesh['y'=4,'zr'=8,'zl'=2,'x'=4,'c'=2] {'y','zl'}, dimensions={0} | all-to-all | bytes 2883584 | tf_op jit(solution)/shard_map/all_to_all | solution.py:33
  228.4 0.0 copy-done.2
  228.4 1.2 apply_update.1
  (9 shorter events, 0.1 us)
Async XLA Ops:
  35.9 8.0 %copy-start = (bf16[576,1408]{1,0:T(8,128)(2,1)S(1)}, bf16[576,1408]{1,0:T(8,128)(2,1)}, u32[]{:S(2)}) copy-start(bf16[576,1408]{1,0:T(8,128)(2,1)} %own_grads.1) | copy-start | bytes 4866052
  37.1 22.4 %all-to-all-start.1 = ((bf16[64,4,16,128]{3,2,1,0:T(8,128)(2,1)}), bf16[64,4,16,128]{3,2,1,0:T(8,128)(2,1)S(1)}, u32[]{:S(2)}, u32[]{:S(2)}) async-start(bf16[64,4,16,128]{3,2,1,0:T(8,128)(2,1)} %bitcast.23), calls=%async_computation.1 | async-start | bytes 2097152 | tf_op jit(solution)/shard_map/all_to_all | solution.py:33
  43.9 48.4 %collective-permute-start = (bf16[576,1408]{1,0:T(8,128)(2,1)S(1)}, bf16[576,1408]{1,0:T(8,128)(2,1)}, u32[]{:S(2)}, u32[]{:S(2)}) collective-permute-start(bf16[576,1408]{1,0:T(8,128)(2,1)S(1)} %copy-done), channel_id=1, source_target_pairs={{0,8},{8,0},{1,9},{9,1},{2,10},{10,2},{3,11},{11,3},{4,12},{12,4},... | collective-permute-start | bytes 4866056 | tf_op jit(solution)/shard_map/ppermute | solution.py:187
  59.5 1.3 copy-start.1
  124.5 63.7 %copy-start.3 = (f32[8,1408]{1,0:T(8,128)S(1)}, f32[8,1408]{1,0:T(8,128)}, u32[]{:S(2)}) copy-start(f32[8,1408]{1,0:T(8,128)} %first_moment.1) | copy-start | bytes 135172
  124.6 63.7 %copy-start.4 = (f32[8,1408]{1,0:T(8,128)S(1)}, f32[8,1408]{1,0:T(8,128)}, u32[]{:S(2)}) copy-start(f32[8,1408]{1,0:T(8,128)} %second_moment.1) | copy-start | bytes 135172
  207.7 20.6 %copy-start.2 = (bf16[128,1408]{1,0:T(8,128)(2,1)S(1)}, bf16[128,1408]{1,0:T(8,128)(2,1)}, u32[]{:S(2)}) copy-start(bf16[128,1408]{1,0:T(8,128)(2,1)} %weight.1) | copy-start | bytes 1081348

commit v4 on v2

v4 whole, which is shorter than its diff:
```python
import math

import jax
import jax.numpy as jnp
from jax import lax
from jax.experimental import pallas as pl
from jax.experimental.pallas import tpu as pltpu
from jax.sharding import Mesh
from jax.sharding import PartitionSpec as P


FW = 11264
R = 512
AXES = ("y", "zr", "zl", "x", "c")
DP = ("y", "zr", "zl")
TENSOR = ("x", "c")
NEAR = ("y", "zl")
PLANE = ("y", "zl", "x", "c")
BF = jnp.bfloat16
F32 = jnp.float32


beta_one = 0.9
beta_two = 0.999
adam_eps = 1e-08
corr_one = 1.0 - 0.9**10
corr_two = 1.0 - 0.999**10
step_size = 0.002
decay_keep = 0.99


def exchange(x, axes):
    return lax.all_to_all(x, axes, split_axis=0, concat_axis=0, tiled=True)


def across(bit):
    return [(i, i ^ bit) for i in range(8)]


def shape(dims, dtype):
    return jax.ShapeDtypeStruct(dims, dtype)


def small(mib):
    return pltpu.CompilerParams(vmem_limit_bytes=mib * 2**20)


def project_kernel(inputs, blocks, out, columns):
    for y in range(4):
        for zl in range(2):
            for high in range(2):
                for mid in range(2):
                    row = 16 * (((y * 2 + zl) * 2 + high) * 2 + mid)
                    for f in range(8):
                        columns[row : row + 16, 128 * f : 128 * f + 128] = blocks[
                            zl * 2 + mid, f % 2, y, high, f // 2
                        ]
    out[...] = lax.dot_general(
        inputs[...], columns[...], (((1,), (1,)), ((), ())), preferred_element_type=F32
    ).astype(BF)


def project(inputs, blocks):
    return pl.pallas_call(
        project_kernel,
        out_shape=shape((576, 512), BF),
        scratch_shapes=[pltpu.VMEM((512, 1024), BF)],
        compiler_params=small(16),
        name="project",
    )(inputs, blocks)


def near_kernel(parts, out):
    out[...] = jnp.sum(parts[...].astype(F32), axis=0).astype(BF)


def near_sum(parts):
    return pl.pallas_call(
        near_kernel,
        out_shape=shape((64, 1408), BF),
        compiler_params=small(8),
        name="near_sum",
    )(parts)


def own_kernel(parts, rows, shared):
    own = jnp.sum(parts[...].astype(F32), axis=0)
    rows[...] = own
    squares = own * own
    lanes = jnp.zeros((1, 128), F32)
    for k in range(11):
        lanes += jnp.sum(squares[:, 128 * k : 128 * k + 128], axis=0, keepdims=True)
    high = lanes.astype(BF).astype(F32)
    at = lax.broadcasted_iota(jnp.int32, (8, 128), 0)
    split = jnp.where(at == 0, high, jnp.where(at == 1, lanes - high, 0.0)).astype(BF)
    rounded = own.astype(BF)
    for k in range(8):
        shared[k, :, :1408] = rounded
        shared[k, :, 1408:] = split


def own_sum(parts):
    return pl.pallas_call(
        own_kernel,
        out_shape=(shape((8, 1408), F32), shape((8, 8, 1536), BF)),
        compiler_params=small(4),
        name="own_sum",
    )(parts)


def far_kernel(shared, out):
    lanes = jnp.sum(jnp.sum(shared[:, :, 1408:].astype(F32), axis=0), axis=0, keepdims=True)
    out[...] = jnp.broadcast_to(lanes[None], (64, 1, 128))


def far_square(shared):
    return pl.pallas_call(
        far_kernel,
        out_shape=shape((64, 1, 128), F32),
        compiler_params=small(2),
        name="far_square",
    )(shared)


def adam_kernel(
    index, lowrank, first_moment, second_moment, square, shared, even, odd, new_first, new_second, update
):
    bound_norm = math.sqrt(R * FW)
    total = jnp.sum(jnp.sum(square[...], axis=0), axis=1, keepdims=True)
    factor = jnp.minimum(1.0, bound_norm / (jnp.sqrt(total) + 1e-06))

    def averages(rows, m, v):
        clipped = rows * factor
        first = beta_one * m + (1.0 - beta_one) * clipped
        return first, beta_two * v + (1.0 - beta_two) * clipped * clipped

    new_first[...], new_second[...] = averages(lowrank[...], first_moment[...], second_moment[...])
    for k in range(8):
        moments = (even, odd)[k % 2]
        at = (k // 2) % 2 * 2 + k // 4
        z = index[0] ^ k
        first, second = averages(
            shared[z, :, :1408].astype(F32), moments[at, 0].astype(F32), moments[at, 1].astype(F32)
        )
        step = (first / corr_one / (jnp.sqrt(second / corr_two) + adam_eps)).astype(BF)
        for copy in range(8):
            update[copy, z] = step


def adam(*args):
    whole = pl.BlockSpec(memory_space=pltpu.VMEM)
    return pl.pallas_call(
        adam_kernel,
        in_specs=[pl.BlockSpec(memory_space=pltpu.SMEM)] + [whole] * 7,
        out_shape=(shape((8, 1408), F32), shape((8, 1408), F32), shape((8, 8, 8, 1408), BF)),
        compiler_params=small(8),
        name="adam",
    )(*args)


def apply_kernel(both, update, decayed, out, back):
    for y in range(4):
        for high in range(2):
            for k in range(4):
                row = ((y * 2 + k // 2) * 2 + high) * 32 + (k % 2) * 16
                back[row : row + 16, :] = both[y * 2 + high, :16, 128 * k : 128 * k + 128]
    delta = lax.dot_general(
        back[...], update[...], (((0,), (0,)), ((), ())), preferred_element_type=F32
    )
    out[...] = (decayed[...] - step_size * delta).astype(BF)


def apply_update(both, update, decayed):
    return pl.pallas_call(
        apply_kernel,
        out_shape=shape((128, 1408), BF),
        scratch_shapes=[pltpu.VMEM((512, 128), BF)],
        compiler_params=small(12),
        name="apply_update",
    )(both, update, decayed)


def body(inputs, out_grads, basis, weight, first_moment, second_moment):
    piece = basis.T.reshape(4, 2, 8, 128).transpose(1, 0, 2, 3).reshape(64, 128)
    quarters = jnp.broadcast_to(piece.reshape(4, 1, 16, 128), (4, 8, 16, 128))
    index = lax.axis_index("zr").reshape(1)
    quarters, index = lax.optimization_barrier((quarters, index))
    far = exchange(quarters.reshape(32, 16, 128), ("y", "zr"))
    copies = jnp.broadcast_to(far.reshape(1, 8, 4, 16, 128), (8, 8, 4, 16, 128))
    slices = exchange(copies.reshape(64, 4, 16, 128), PLANE)
    partial_value = project(inputs, slices.reshape(4, 2, 4, 2, 4, 16, 128))
    shares = exchange(partial_value.reshape(8, 72, 512), TENSOR)
    wide = jnp.concatenate([piece[16 * k : 16 * k + 16] for k in range(4)], axis=1)
    moments = jnp.stack([first_moment, second_moment]).astype(BF)
    other = lax.ppermute(moments, "zr", across(4))
    moments = jnp.stack([moments, other])
    second = lax.ppermute(moments, "zr", across(2))
    own_tokens = jnp.sum(shares.astype(F32), axis=0).astype(BF)
    own_tokens = jnp.broadcast_to(jnp.concatenate([wide, own_tokens], axis=0), (8, 88, 512))
    both = exchange(own_tokens, TENSOR)
    decayed = decay_keep * weight.astype(F32)
    projected = both[:, 16:].reshape(576, 512)
    partial_low = lax.dot_general(
        projected, out_grads, (((0,), (0,)), ((), ())), preferred_element_type=F32
    ).astype(BF)
    near = exchange(partial_low.reshape(8, 64, 1408), NEAR)
    own = exchange(near_sum(near).reshape(8, 8, 1408), ("zr",))
    own_rows, shared = own_sum(own)
    shared = exchange(shared, ("zr",))
    square = far_square(shared)
    square = exchange(square, PLANE)
    even = jnp.concatenate([moments, second])
    odd = lax.ppermute(even, "zr", across(1))
    first, second, update = adam(index, own_rows, first_moment, second_moment, square, shared, even, odd)
    all_update = exchange(update.reshape(8, 64, 1408), NEAR).reshape(512, 1408)
    new_weight = apply_update(both, all_update, decayed)
    return (new_weight, first, second)


def solution(mesh):
    torus = Mesh(mesh.devices.reshape(4, 8, 2, 4, 2), AXES)
    spec = P(DP, TENSOR)
    return jax.shard_map(
        body,
        mesh=torus,
        in_specs=(spec,) * 6,
        out_specs=(spec,) * 3,
        check_vma=False,
    )
```

time: 202 us -> 220 us (1.089)
  blocking collectives: 195 us -> 94.1 us
  waiting for transfers between devices: 0 us -> 65.7 us
  starting transfers between devices: 0 us -> 43.4 us
  local copies, waits for them, and re-layouts: 1.33 us -> 5.4 us
  Pallas kernels: 3.1 us -> 6.12 us
    all_to_all x10 -> x4, blocking collectives: 195 us -> 94.1 us  [exchange(): return lax.all_to_all(x, axes, split_axis=0, concat_axis=0, tiled=True)]
    all_to_all x0 -> x5, waiting for transfers between devices: none -> 50.8 us  [exchange(): return lax.all_to_all(x, axes, split_axis=0, concat_axis=0, tiled=True)]
    all_to_all x0 -> x5, starting transfers between devices: none -> 24.5 us  [exchange(): return lax.all_to_all(x, axes, split_axis=0, concat_axis=0, tiled=True)]
    ppermute x0 -> x3, starting transfers between devices: none -> 18.9 us  [the longest x1 12.6 us: body(): other = lax.ppermute(moments, 'zr', across(4))]
    ppermute x0 -> x3, waiting for transfers between devices: none -> 14.9 us  [the longest x1 8.73 us: body(): second = lax.ppermute(moments, 'zr', across(2))]
    unnamed x10 -> x18, local copies, waits for them, and re-layouts: 0.03 us -> 4.21 us
  transfers between devices with their start and end apart: 0 -> 8, of which waited for: 0 -> 6; matrix products, arithmetic and copies ran while one was open for 0% -> 0% of each run, Pallas kernels for 0% -> 0%
where the time goes in v4:
time: 220 us; the launch traced here: 218 us
  blocking collectives  94.1 us (43%)
  waiting for transfers between devices  65.7 us (30%)
  starting transfers between devices  43.4 us (20%)
  Pallas kernels  6.12 us (3%)
  local copies, waits for them, and re-layouts  5.4 us (2%)
    all_to_all x4, blocking collectives, exchange(): return lax.all_to_all(x, axes, split_axis=0, concat_axis=0, tiled=True)  94.1 us
    all_to_all x5, waiting for transfers between devices, exchange(): return lax.all_to_all(x, axes, split_axis=0, concat_axis=0, tiled=True)  50.8 us
    all_to_all x5, starting transfers between devices, exchange(): return lax.all_to_all(x, axes, split_axis=0, concat_axis=0, tiled=True)  24.5 us
    ppermute x1, starting transfers between devices, body(): other = lax.ppermute(moments, 'zr', across(4))  12.6 us
    ppermute x1, waiting for transfers between devices, body(): second = lax.ppermute(moments, 'zr', across(2))  8.73 us
    ppermute x1, waiting for transfers between devices, body(): other = lax.ppermute(moments, 'zr', across(4))  6.17 us
  transfers between devices with their start and end apart: 8, of which 6 were waited for; matrix products, arithmetic and copies ran while one was open for 0% of the time, Pallas kernels for 0%

profile of v4, /device:TPU:6, one launch (start us, length us, event | category | flops | bytes accessed | tf_op | source)
XLA Modules:
  0.0 218.1 jit_solution(10526975018551567309)
XLA Ops:
  0.6 0.8 copy.11
  1.5 34.5 %all_to_all.45 = bf16[32,16,128]{2,1,0:T(8,128)(2,1)S(1)} all-to-all(bf16[32,16,128]{2,1,0:T(8,128)(2,1)S(1)} %bitcast.36), channel_id=1, replica_groups=mesh['y'=4,'zr'=8,'zl'=2,'x'=4,'c'=2] {'y','zr'}, dimensions={0} | all-to-all | bytes 262144 | tf_op jit(solution)/shard_map/all_to_all | solution.py:33
  36.0 0.2 broadcast_in_dim.20
  36.3 21.9 %all_to_all.46 = bf16[64,4,16,128]{3,2,1,0:T(8,128)(2,1)S(1)} all-to-all(bf16[64,4,16,128]{3,2,1,0:T(8,128)(2,1)S(1)} %bitcast.32), channel_id=1, replica_groups=mesh['y'=4,'zr'=8,'zl'=2,'x'=4,'c'=2] {'y','zl','x','c'}, dimensions={0} | all-to-all | bytes 2097152 | tf_op jit(solution)/shard_map/all_to_all | solution.py:33
  58.2 1.7 project.1
  59.9 6.5 %all-to-all-start.2 = ((bf16[8,72,512]{2,1,0:T(8,128)(2,1)}), bf16[8,72,512]{2,1,0:T(8,128)(2,1)S(1)}, u32[]{:S(2)}, u32[]{:S(2)}) async-start(bf16[8,72,512]{2,1,0:T(8,128)(2,1)} %bitcast.12), calls=%async_computation.2 | async-start | bytes 1179648 | tf_op jit(solution)/shard_map/all_to_all | solution.py:33
  66.4 8.9 %all-to-all-done.2 = bf16[8,72,512]{2,1,0:T(8,128)(2,1)S(1)} async-done(((bf16[8,72,512]{2,1,0:T(8,128)(2,1)}), bf16[8,72,512]{2,1,0:T(8,128)(2,1)S(1)}, u32[]{:S(2)}, u32[]{:S(2)}) %all-to-all-start.2) | async-done | bytes 589856 | tf_op jit(solution)/shard_map/all_to_all | solution.py:33
  75.5 14.9 %all_to_all.47.both = bf16[8,88,512]{2,1,0:T(8,128)(2,1)S(1)} all-to-all(bf16[8,88,512]{2,1,0:T(8,128)(2,1)S(1)} %broadcast_in_dim.21), channel_id=1, replica_groups=mesh['y'=4,'zr'=8,'zl'=2,'x'=4,'c'=2] {'x','c'}, dimensions={0} | all-to-all | bytes 1441792 | tf_op jit(solution)/shard_map/all_to_all | solution.py:33
  90.4 0.8 copy-done.1
  91.2 1.4 convolution_convert_fusion
  92.6 22.8 %all_to_all.48.parts = bf16[8,64,1408]{2,1,0:T(8,128)(2,1)S(1)} all-to-all(bf16[8,64,1408]{2,1,0:T(8,128)(2,1)S(1)} %bitcast.33), channel_id=1, replica_groups=mesh['y'=4,'zr'=8,'zl'=2,'x'=4,'c'=2] {'y','zl'}, dimensions={0} | all-to-all | bytes 2883584 | tf_op jit(solution)/shard_map/all_to_all | solution.py:33
  115.5 0.9 near_sum.1
  116.3 3.4 %all-to-all-start.5 = ((bf16[8,8,1408]{2,1,0:T(8,128)(2,1)}), bf16[8,8,1408]{2,1,0:T(8,128)(2,1)S(1)}, u32[]{:S(2)}, u32[]{:S(2)}) async-start(bf16[8,8,1408]{2,1,0:T(8,128)(2,1)} %bitcast.15), calls=%async_computation.5 | async-start | bytes 360448 | tf_op jit(solution)/shard_map/all_to_all | solution.py:33
  119.8 16.2 %all-to-all-done.5.parts = bf16[8,8,1408]{2,1,0:T(8,128)(2,1)S(1)} async-done(((bf16[8,8,1408]{2,1,0:T(8,128)(2,1)}), bf16[8,8,1408]{2,1,0:T(8,128)(2,1)S(1)}, u32[]{:S(2)}, u32[]{:S(2)}) %all-to-all-start.5) | async-done | bytes 180256 | tf_op jit(solution)/shard_map/all_to_all | solution.py:33
  136.0 0.7 own_sum.1
  136.7 3.4 %all-to-all-start.6 = ((bf16[8,8,1536]{2,1,0:T(8,128)(2,1)}), bf16[8,8,1536]{2,1,0:T(8,128)(2,1)S(1)}, u32[]{:S(2)}, u32[]{:S(2)}) async-start(bf16[8,8,1536]{2,1,0:T(8,128)(2,1)} %get-tuple-element.13), calls=%async_computation.6 | async-start | bytes 393216 | tf_op jit(solution)/shard_map/all_to_all | solution.py:33
  140.1 12.6 %collective-permute-start = (bf16[2,8,1408]{2,1,0:T(8,128)(2,1)S(1)}, bf16[2,8,1408]{2,1,0:T(8,128)(2,1)S(1)}, u32[]{:S(2)}, u32[]{:S(2)}) collective-permute-start(bf16[2,8,1408]{2,1,0:T(8,128)(2,1)S(1)} %pad_maximum_fusion.3), channel_id=1, source_target_pairs={{0,64},{16,80},{32,96},{48,112},{64,0},{80,16},{96,32},{112,48},{1... | collective-permute-start | bytes 135176 | tf_op jit(solution)/shard_map/ppermute | solution.py:195
  152.7 6.2 %collective-permute-done = bf16[2,8,1408]{2,1,0:T(8,128)(2,1)S(1)} collective-permute-done((bf16[2,8,1408]{2,1,0:T(8,128)(2,1)S(1)}, bf16[2,8,1408]{2,1,0:T(8,128)(2,1)S(1)}, u32[]{:S(2)}, u32[]{:S(2)}) %collective-permute-start) | collective-permute-done | bytes 45088 | tf_op jit(solution)/shard_map/ppermute | solution.py:195
  158.9 4.3 %collective-permute-start.1 = (bf16[2,2,8,1408]{3,2,1,0:T(8,128)(2,1)S(1)}, bf16[2,2,8,1408]{3,2,1,0:T(8,128)(2,1)S(1)}, u32[]{:S(2)}, u32[]{:S(2)}) collective-permute-start(bf16[2,2,8,1408]{3,2,1,0:T(8,128)(2,1)S(1)} %pad_maximum_fusion.2), channel_id=1, source_target_pairs={{0,32},{16,48},{32,0},{48,16},{64,96},{80,112},{96,64},{112,80},{1... | collective-permute-start | bytes 270344 | tf_op jit(solution)/shard_map/ppermute | solution.py:197
  163.2 8.7 %collective-permute-done.1 = bf16[2,2,8,1408]{3,2,1,0:T(8,128)(2,1)S(1)} collective-permute-done((bf16[2,2,8,1408]{3,2,1,0:T(8,128)(2,1)S(1)}, bf16[2,2,8,1408]{3,2,1,0:T(8,128)(2,1)S(1)}, u32[]{:S(2)}, u32[]{:S(2)}) %collective-permute-start.1) | collective-permute-done | bytes 90144 | tf_op jit(solution)/shard_map/ppermute | solution.py:197
  172.0 2.0 collective-permute-start.2
  174.0 0.6 far_square.1
  174.6 7.6 %all-to-all-start.7 = ((f32[64,1,128]{2,1,0:T(1,128)}), f32[64,1,128]{2,1,0:T(1,128)S(1)}, u32[]{:S(2)}, u32[]{:S(2)}) async-start(f32[64,1,128]{2,1,0:T(1,128)} %far_square.1), calls=%async_computation.7 | async-start | bytes 65536 | tf_op jit(solution)/shard_map/all_to_all | solution.py:33
  182.2 6.4 %all-to-all-done.7.square = f32[64,1,128]{2,1,0:T(1,128)S(1)} async-done(((f32[64,1,128]{2,1,0:T(1,128)}), f32[64,1,128]{2,1,0:T(1,128)S(1)}, u32[]{:S(2)}, u32[]{:S(2)}) %all-to-all-start.7) | async-done | bytes 32800 | tf_op jit(solution)/shard_map/all_to_all | solution.py:33
  188.6 1.0 adam.1
  189.7 1.1 copy-done.4
  190.8 3.7 %all-to-all-start.8 = ((bf16[8,64,1408]{2,1,0:T(8,128)(2,1)}), bf16[8,64,1408]{2,1,0:T(8,128)(2,1)S(1)}, u32[]{:S(2)}, u32[]{:S(2)}) async-start(bf16[8,64,1408]{2,1,0:T(8,128)(2,1)} %bitcast.31), calls=%async_computation.8 | async-start | bytes 2883584 | tf_op jit(solution)/shard_map/all_to_all | solution.py:33
  194.5 0.9 convert_multiply_fusion.decayed
  195.4 19.3 %all-to-all-done.8 = bf16[8,64,1408]{2,1,0:T(8,128)(2,1)S(1)} async-done(((bf16[8,64,1408]{2,1,0:T(8,128)(2,1)}), bf16[8,64,1408]{2,1,0:T(8,128)(2,1)S(1)}, u32[]{:S(2)}, u32[]{:S(2)}) %all-to-all-start.8) | async-done | bytes 1441824 | tf_op jit(solution)/shard_map/all_to_all | solution.py:33
  214.7 1.1 copy-done.2
  215.8 1.1 copy-done.3
  216.9 1.1 apply_update.1
  (26 shorter events, 0.3 us)
Async XLA Ops:
  0.6 90.6 %copy-start = (bf16[576,1408]{1,0:T(8,128)(2,1)S(1)}, bf16[576,1408]{1,0:T(8,128)(2,1)}, u32[]{:S(2)}) copy-start(bf16[576,1408]{1,0:T(8,128)(2,1)} %param.7) | copy-start | bytes 4866052
  36.0 22.2 %copy-start.5 = (bf16[576,1024]{1,0:T(8,128)(2,1)S(1)}, bf16[576,1024]{1,0:T(8,128)(2,1)}, u32[]{:S(2)}) copy-start(bf16[576,1024]{1,0:T(8,128)(2,1)} %inputs.1) | copy-start | bytes 3538948
  59.9 15.4 %all-to-all-start.2 = ((bf16[8,72,512]{2,1,0:T(8,128)(2,1)}), bf16[8,72,512]{2,1,0:T(8,128)(2,1)S(1)}, u32[]{:S(2)}, u32[]{:S(2)}) async-start(bf16[8,72,512]{2,1,0:T(8,128)(2,1)} %bitcast.12), calls=%async_computation.2 | async-start | bytes 1179648 | tf_op jit(solution)/shard_map/all_to_all | solution.py:33
  90.4 0.8 copy-start.1
  115.5 4.3 %copy-start.6 = (f32[8,1408]{1,0:T(8,128)S(1)}, f32[8,1408]{1,0:T(8,128)}, u32[]{:S(2)}) copy-start(f32[8,1408]{1,0:T(8,128)} %first_moment.1) | copy-start | bytes 135172
  115.5 4.3 %copy-start.7 = (f32[8,1408]{1,0:T(8,128)S(1)}, f32[8,1408]{1,0:T(8,128)}, u32[]{:S(2)}) copy-start(f32[8,1408]{1,0:T(8,128)} %second_moment.1) | copy-start | bytes 135172
  116.3 19.6 %all-to-all-start.5 = ((bf16[8,8,1408]{2,1,0:T(8,128)(2,1)}), bf16[8,8,1408]{2,1,0:T(8,128)(2,1)S(1)}, u32[]{:S(2)}, u32[]{:S(2)}) async-start(bf16[8,8,1408]{2,1,0:T(8,128)(2,1)} %bitcast.15), calls=%async_computation.5 | async-start | bytes 360448 | tf_op jit(solution)/shard_map/all_to_all | solution.py:33
  136.7 37.3 %all-to-all-start.6 = ((bf16[8,8,1536]{2,1,0:T(8,128)(2,1)}), bf16[8,8,1536]{2,1,0:T(8,128)(2,1)S(1)}, u32[]{:S(2)}, u32[]{:S(2)}) async-start(bf16[8,8,1536]{2,1,0:T(8,128)(2,1)} %get-tuple-element.13), calls=%async_computation.6 | async-start | bytes 393216 | tf_op jit(solution)/shard_map/all_to_all | solution.py:33
  140.1 18.7 %collective-permute-start = (bf16[2,8,1408]{2,1,0:T(8,128)(2,1)S(1)}, bf16[2,8,1408]{2,1,0:T(8,128)(2,1)S(1)}, u32[]{:S(2)}, u32[]{:S(2)}) collective-permute-start(bf16[2,8,1408]{2,1,0:T(8,128)(2,1)S(1)} %pad_maximum_fusion.3), channel_id=1, source_target_pairs={{0,64},{16,80},{32,96},{48,112},{64,0},{80,16},{96,32},{112,48},{1... | collective-permute-start | bytes 135176 | tf_op jit(solution)/shard_map/ppermute | solution.py:195
  158.9 13.1 %collective-permute-start.1 = (bf16[2,2,8,1408]{3,2,1,0:T(8,128)(2,1)S(1)}, bf16[2,2,8,1408]{3,2,1,0:T(8,128)(2,1)S(1)}, u32[]{:S(2)}, u32[]{:S(2)}) collective-permute-start(bf16[2,2,8,1408]{3,2,1,0:T(8,128)(2,1)S(1)} %pad_maximum_fusion.2), channel_id=1, source_target_pairs={{0,32},{16,48},{32,0},{48,16},{64,96},{80,112},{96,64},{112,80},{1... | collective-permute-start | bytes 270344 | tf_op jit(solution)/shard_map/ppermute | solution.py:197
  172.0 10.2 %collective-permute-start.2 = (bf16[4,2,8,1408]{3,2,1,0:T(8,128)(2,1)S(1)}, bf16[4,2,8,1408]{3,2,1,0:T(8,128)(2,1)S(1)}, u32[]{:S(2)}, u32[]{:S(2)}) collective-permute-start(bf16[4,2,8,1408]{3,2,1,0:T(8,128)(2,1)S(1)} %pad_maximum_fusion.even), channel_id=1, source_target_pairs={{0,16},{16,0},{32,48},{48,32},{64,80},{80,64},{96,112},{112,96},{1... | collective-permute-start | bytes 540680 | tf_op jit(solution)/shard_map/ppermute | solution.py:213
  174.6 14.0 %all-to-all-start.7 = ((f32[64,1,128]{2,1,0:T(1,128)}), f32[64,1,128]{2,1,0:T(1,128)S(1)}, u32[]{:S(2)}, u32[]{:S(2)}) async-start(f32[64,1,128]{2,1,0:T(1,128)} %far_square.1), calls=%async_computation.7 | async-start | bytes 65536 | tf_op jit(solution)/shard_map/all_to_all | solution.py:33
  189.7 1.1 copy-start.4
  190.8 3.7 %copy-start.8 = (bf16[128,1408]{1,0:T(8,128)(2,1)S(1)}, bf16[128,1408]{1,0:T(8,128)(2,1)}, u32[]{:S(2)}) copy-start(bf16[128,1408]{1,0:T(8,128)(2,1)} %param.9) | copy-start | bytes 1081348
  190.8 23.9 %all-to-all-start.8 = ((bf16[8,64,1408]{2,1,0:T(8,128)(2,1)}), bf16[8,64,1408]{2,1,0:T(8,128)(2,1)S(1)}, u32[]{:S(2)}, u32[]{:S(2)}) async-start(bf16[8,64,1408]{2,1,0:T(8,128)(2,1)} %bitcast.31), calls=%async_computation.8 | async-start | bytes 2883584 | tf_op jit(solution)/shard_map/all_to_all | solution.py:33
  214.7 1.1 copy-start.2
  215.8 1.1 copy-start.3

commit v5 on v2

--- a/solution.py
+++ b/solution.py
@@ -13,7 +13,8 @@
 AXES = ("y", "zr", "zl", "x", "c")
 DP = ("y", "zr", "zl")
 TENSOR = ("x", "c")
-NEAR = ("y", "zl")
+SHARES = ("c", "x")
+NEAR = ("zl", "y")
 PLANE = ("y", "zl", "x", "c")
 BF = jnp.bfloat16
 F32 = jnp.float32
@@ -46,11 +47,11 @@
 
 
 def project_kernel(inputs, blocks, out, columns):
-    for y in range(4):
-        for zl in range(2):
+    for zl in range(2):
+        for y in range(4):
             for high in range(2):
                 for mid in range(2):
-                    row = 16 * (((y * 2 + zl) * 2 + high) * 2 + mid)
+                    row = 16 * (((zl * 4 + y) * 2 + high) * 2 + mid)
                     for f in range(8):
                         columns[row : row + 16, 128 * f : 128 * f + 128] = blocks[
                             zl * 2 + mid, f % 2, y, high, f // 2
@@ -143,8 +144,8 @@
     for y in range(4):
         for high in range(2):
             for k in range(4):
-                row = ((y * 2 + k // 2) * 2 + high) * 32 + (k % 2) * 16
-                back[row : row + 16, :] = both[y * 2 + high, :16, 128 * k : 128 * k + 128]
+                row = ((k // 2 * 4 + y) * 2 + high) * 32 + (k % 2) * 16
+                back[row : row + 16, :] = both[high * 4 + y, :16, 128 * k : 128 * k + 128]
     delta = lax.dot_general(
         back[...], update[...], (((0,), (0,)), ((), ())), preferred_element_type=F32
     )
@@ -170,9 +171,9 @@
     copies = jnp.broadcast_to(far.reshape(1, 8, 4, 16, 128), (8, 8, 4, 16, 128))
     slices = exchange(copies.reshape(64, 4, 16, 128), PLANE)
     partial_value = project(inputs, slices.reshape(4, 2, 4, 2, 4, 16, 128))
-    shares = exchange(partial_value.reshape(8, 72, 512), TENSOR)
+    shares = exchange(partial_value.reshape(8, 72, 512), SHARES)
     own_tokens = jnp.sum(shares.astype(F32), axis=0).astype(BF)
-    both = to_all(jnp.concatenate([wide, own_tokens], axis=0), TENSOR)
+    both = to_all(jnp.concatenate([wide, own_tokens], axis=0), SHARES)
     projected = both[:, 16:].reshape(576, 512)
     partial_low = lax.dot_general(
         projected, out_grads, (((0,), (0,)), ((), ())), preferred_element_type=F32

time: 202 us -> 202 us (level)
  no operation moved by 1% of the time
where the time goes in v5:
time: 202 us; the launch traced here: 201 us
  blocking collectives  195 us (97%)
  Pallas kernels  3.09 us (2%)
    all_to_all x10, blocking collectives, exchange(): return lax.all_to_all(x, axes, split_axis=0, concat_axis=0, tiled=True)  195 us

profile of v5, /device:TPU:6, one launch (start us, length us, event | category | flops | bytes accessed | tf_op | source)
XLA Modules:
  0.0 201.3 jit_solution(16923756411182509359)
XLA Ops:
  0.6 0.0 copy-start
  0.6 0.8 copy.11
  1.5 34.5 %all_to_all.50 = bf16[32,16,128]{2,1,0:T(8,128)(2,1)S(1)} all-to-all(bf16[32,16,128]{2,1,0:T(8,128)(2,1)S(1)} %bitcast.28), channel_id=1, replica_groups=mesh['y'=4,'zr'=8,'zl'=2,'x'=4,'c'=2] {'y','zr'}, dimensions={0} | all-to-all | bytes 262144 | tf_op jit(solution)/shard_map/all_to_all | solution.py:33
  36.0 0.0 copy-start.1
  36.0 0.2 broadcast_in_dim.23
  36.3 21.9 %all_to_all.51 = bf16[64,4,16,128]{3,2,1,0:T(8,128)(2,1)S(1)} all-to-all(bf16[64,4,16,128]{3,2,1,0:T(8,128)(2,1)S(1)} %bitcast.23), channel_id=1, replica_groups=mesh['y'=4,'zr'=8,'zl'=2,'x'=4,'c'=2] {'y','zl','x','c'}, dimensions={0} | all-to-all | bytes 2097152 | tf_op jit(solution)/shard_map/all_to_all | solution.py:33
  58.2 0.0 copy-done.1
  58.2 0.9 project.1
  59.1 14.5 %all_to_all.52 = bf16[8,72,512]{2,1,0:T(8,128)(2,1)S(1)} all-to-all(bf16[8,72,512]{2,1,0:T(8,128)(2,1)S(1)} %bitcast.21), channel_id=1, replica_groups=mesh['y'=4,'zr'=8,'zl'=2,'x'=4,'c'=2] {'c','x'}, dimensions={0} | all-to-all | bytes 1179648 | tf_op jit(solution)/shard_map/all_to_all | solution.py:33
  73.6 0.1 reduce_sum.12
  73.8 14.7 %all_to_all.53.both = bf16[8,88,512]{2,1,0:T(8,128)(2,1)S(1)} all-to-all(bf16[8,88,512]{2,1,0:T(8,128)(2,1)S(1)} %broadcast_in_dim.24), channel_id=1, replica_groups=mesh['y'=4,'zr'=8,'zl'=2,'x'=4,'c'=2] {'c','x'}, dimensions={0} | all-to-all | bytes 1441792 | tf_op jit(solution)/shard_map/all_to_all | solution.py:33
  88.5 0.0 copy-done
  88.5 1.4 convolution_convert_fusion
  89.9 22.5 %all_to_all.54.parts = bf16[8,64,1408]{2,1,0:T(8,128)(2,1)S(1)} all-to-all(bf16[8,64,1408]{2,1,0:T(8,128)(2,1)S(1)} %bitcast.24), channel_id=1, replica_groups=mesh['y'=4,'zr'=8,'zl'=2,'x'=4,'c'=2] {'zl','y'}, dimensions={0} | all-to-all | bytes 2883584 | tf_op jit(solution)/shard_map/all_to_all | solution.py:33
  112.4 0.0 copy-start.3
  112.4 0.0 copy-start.4
  112.4 0.2 near_sum.1
  112.6 18.3 %all_to_all.55.parts = bf16[8,8,1408]{2,1,0:T(8,128)(2,1)S(1)} all-to-all(bf16[8,8,1408]{2,1,0:T(8,128)(2,1)S(1)} %bitcast.22), channel_id=1, replica_groups=mesh['y'=4,'zr'=8,'zl'=2,'x'=4,'c'=2] {'zr'}, dimensions={0} | all-to-all | bytes 360448 | tf_op jit(solution)/shard_map/all_to_all | solution.py:33
  131.0 0.1 own_sum.1
  131.0 13.7 %all_to_all.56.parts = f32[64,1,128]{2,1,0:T(1,128)S(1)} all-to-all(f32[64,1,128]{2,1,0:T(1,128)S(1)} %get-tuple-element.13), channel_id=1, replica_groups=mesh['y'=4,'zr'=8,'zl'=2,'x'=4,'c'=2] {'y','zl','x','c'}, dimensions={0} | all-to-all | bytes 65536 | tf_op jit(solution)/shard_map/all_to_all | solution.py:33
  144.7 0.1 plane_sum.1
  144.8 15.3 %all_to_all.57.square = f32[8,1,128]{2,1,0:T(1,128)S(1)} all-to-all(f32[8,1,128]{2,1,0:T(1,128)S(1)} %plane_sum.1), channel_id=1, replica_groups=mesh['y'=4,'zr'=8,'zl'=2,'x'=4,'c'=2] {'zr'}, dimensions={0} | all-to-all | bytes 8192 | tf_op jit(solution)/shard_map/all_to_all | solution.py:33
  160.1 0.0 copy-done.3
  160.1 0.0 copy-done.4
  160.1 0.7 adam.1
  160.9 18.7 %all_to_all.58 = bf16[8,8,1408]{2,1,0:T(8,128)(2,1)S(1)} all-to-all(bf16[8,8,1408]{2,1,0:T(8,128)(2,1)S(1)} %get-tuple-element.14), channel_id=1, replica_groups=mesh['y'=4,'zr'=8,'zl'=2,'x'=4,'c'=2] {'zr'}, dimensions={0} | all-to-all | bytes 360448 | tf_op jit(solution)/shard_map/all_to_all | solution.py:33
  179.5 0.1 broadcast_in_dim.25
  179.6 0.0 copy-start.2
  179.7 20.5 %all_to_all.59 = bf16[8,64,1408]{2,1,0:T(8,128)(2,1)S(1)} all-to-all(bf16[8,64,1408]{2,1,0:T(8,128)(2,1)S(1)} %broadcast_in_dim.25), channel_id=1, replica_groups=mesh['y'=4,'zr'=8,'zl'=2,'x'=4,'c'=2] {'zl','y'}, dimensions={0} | all-to-all | bytes 2883584 | tf_op jit(solution)/shard_map/all_to_all | solution.py:33
  200.2 0.0 copy-done.2
  200.2 1.2 apply_update.1
  (6 shorter events, 0.1 us)
Async XLA Ops:
  0.6 87.9 %copy-start = (bf16[576,1408]{1,0:T(8,128)(2,1)S(1)}, bf16[576,1408]{1,0:T(8,128)(2,1)}, u32[]{:S(2)}) copy-start(bf16[576,1408]{1,0:T(8,128)(2,1)} %param.7) | copy-start | bytes 4866052
  36.0 22.2 %copy-start.1 = (bf16[576,1024]{1,0:T(8,128)(2,1)S(1)}, bf16[576,1024]{1,0:T(8,128)(2,1)}, u32[]{:S(2)}) copy-start(bf16[576,1024]{1,0:T(8,128)(2,1)} %inputs.1) | copy-start | bytes 3538948
  112.4 47.7 %copy-start.3 = (f32[8,1408]{1,0:T(8,128)S(1)}, f32[8,1408]{1,0:T(8,128)}, u32[]{:S(2)}) copy-start(f32[8,1408]{1,0:T(8,128)} %first_moment.1) | copy-start | bytes 135172
  112.4 47.7 %copy-start.4 = (f32[8,1408]{1,0:T(8,128)S(1)}, f32[8,1408]{1,0:T(8,128)}, u32[]{:S(2)}) copy-start(f32[8,1408]{1,0:T(8,128)} %second_moment.1) | copy-start | bytes 135172
  179.6 20.5 %copy-start.2 = (bf16[128,1408]{1,0:T(8,128)(2,1)S(1)}, bf16[128,1408]{1,0:T(8,128)(2,1)}, u32[]{:S(2)}) copy-start(bf16[128,1408]{1,0:T(8,128)(2,1)} %weight.1) | copy-start | bytes 1081348

commit v6 on v5

--- a/solution.py
+++ b/solution.py
@@ -91,13 +91,13 @@
     squares = own * own
     for k in range(11):
         lanes += jnp.sum(squares[:, 128 * k : 128 * k + 128], axis=0, keepdims=True)
-    square[...] = jnp.broadcast_to(lanes[None], (64, 1, 128))
+    square[...] = jnp.broadcast_to(lanes[None], (32, 1, 128))
 
 
 def own_sum(parts):
     return pl.pallas_call(
         own_kernel,
-        out_shape=(shape((8, 1408), F32), shape((64, 1, 128), F32)),
+        out_shape=(shape((8, 1408), F32), shape((32, 1, 128), F32)),
         compiler_params=small(4),
         name="own_sum",
     )(parts)
@@ -105,42 +105,47 @@
 
 def plane_kernel(parts, out):
     total = jnp.sum(parts[...], axis=0, keepdims=True)
-    out[...] = jnp.broadcast_to(total, (8, 1, 128))
+    out[...] = jnp.broadcast_to(total, (16, 1, 128))
 
 
 def plane_sum(parts):
     return pl.pallas_call(
         plane_kernel,
-        out_shape=shape((8, 1, 128), F32),
+        out_shape=shape((16, 1, 128), F32),
         compiler_params=small(2),
         name="plane_sum",
     )(parts)
 
 
-def adam_kernel(lowrank, square, first_moment, second_moment, new_first, new_second, update):
+def averages(lowrank, square, first_moment, second_moment):
     bound_norm = math.sqrt(R * FW)
     total = jnp.sum(jnp.sum(square[...], axis=0), axis=1, keepdims=True)
     factor = jnp.minimum(1.0, bound_norm / (jnp.sqrt(total) + 1e-06))
     clipped = lowrank[...] * factor
     first = beta_one * first_moment[...] + (1.0 - beta_one) * clipped
     second = beta_two * second_moment[...] + (1.0 - beta_two) * clipped * clipped
-    new_first[...] = first
-    new_second[...] = second
+    return first, second
+
+
+def adam_kernel(lowrank, square, first_moment, second_moment, update):
+    first, second = averages(lowrank, square, first_moment, second_moment)
     step = (first / corr_one / (jnp.sqrt(second / corr_two) + adam_eps)).astype(BF)
     for k in range(8):
         update[k] = step
 
 
-def adam(lowrank, square, first_moment, second_moment):
+def adam(*args):
     return pl.pallas_call(
         adam_kernel,
-        out_shape=(shape((8, 1408), F32), shape((8, 1408), F32), shape((8, 8, 1408), BF)),
+        out_shape=shape((8, 8, 1408), BF),
         compiler_params=small(4),
         name="adam",
-    )(lowrank, square, first_moment, second_moment)
-
-
-def apply_kernel(both, update, weight, out, back):
+    )(*args)
+
+
+def apply_kernel(
+    both, update, weight, lowrank, square, first_moment, second_moment, out, new_first, new_second, back
+):
     for y in range(4):
         for high in range(2):
             for k in range(4):
@@ -150,16 +155,17 @@
         back[...], update[...], (((0,), (0,)), ((), ())), preferred_element_type=F32
     )
     out[...] = (decay_keep * weight[...].astype(F32) - step_size * delta).astype(BF)
-
-
-def apply_update(both, update, weight):
+    new_first[...], new_second[...] = averages(lowrank, square, first_moment, second_moment)
+
+
+def apply_update(*args):
     return pl.pallas_call(
         apply_kernel,
-        out_shape=shape((128, 1408), BF),
+        out_shape=(shape((128, 1408), BF), shape((8, 1408), F32), shape((8, 1408), F32)),
         scratch_shapes=[pltpu.VMEM((512, 128), BF)],
         compiler_params=small(12),
         name="apply_update",
-    )(both, update, weight)
+    )(*args)
 
 
 def on_device(inputs, out_grads, basis, weight, first_moment, second_moment):
@@ -181,12 +187,12 @@
     near = exchange(partial_low.reshape(8, 64, 1408), NEAR)
     own = exchange(near_sum(near).reshape(8, 8, 1408), ("zr",))
     own_rows, square = own_sum(own)
-    square = plane_sum(exchange(square, PLANE))
-    first, second, update = adam(own_rows, exchange(square, ("zr",)), first_moment, second_moment)
+    square = plane_sum(exchange(square, ("y", "x", "c")))
+    square = exchange(square, ("zr", "zl"))
+    update = adam(own_rows, square, first_moment, second_moment)
     far_update = exchange(update, ("zr",)).reshape(64, 1408)
     all_update = to_all(far_update, NEAR).reshape(512, 1408)
-    new_weight = apply_update(both, all_update, weight)
-    return (new_weight, first, second)
+    return apply_update(both, all_update, weight, own_rows, square, first_moment, second_moment)
 
 
 def solution(mesh):

time: 202 us -> 200 us (0.990)
    all_to_all x10, blocking collectives: 195 us -> 193 us  [exchange(): return lax.all_to_all(x, axes, split_axis=0, concat_axis=0, tiled=True)]
where the time goes in v6:
time: 200 us; the launch traced here: 199 us
  blocking collectives  193 us (96%)
  Pallas kernels  2.46 us (1%)
    all_to_all x10, blocking collectives, exchange(): return lax.all_to_all(x, axes, split_axis=0, concat_axis=0, tiled=True)  193 us

profile of v6, /device:TPU:6, one launch (start us, length us, event | category | flops | bytes accessed | tf_op | source)
XLA Modules:
  0.0 198.6 jit_solution(11547891345111001419)
XLA Ops:
  0.6 0.0 copy-start
  0.6 0.8 copy.11
  1.5 34.5 %all_to_all.50 = bf16[32,16,128]{2,1,0:T(8,128)(2,1)S(1)} all-to-all(bf16[32,16,128]{2,1,0:T(8,128)(2,1)S(1)} %bitcast.28), channel_id=1, replica_groups=mesh['y'=4,'zr'=8,'zl'=2,'x'=4,'c'=2] {'y','zr'}, dimensions={0} | all-to-all | bytes 262144 | tf_op jit(solution)/shard_map/all_to_all | solution.py:33
  36.0 0.0 copy-start.1
  36.0 0.2 broadcast_in_dim.23
  36.3 21.9 %all_to_all.51 = bf16[64,4,16,128]{3,2,1,0:T(8,128)(2,1)S(1)} all-to-all(bf16[64,4,16,128]{3,2,1,0:T(8,128)(2,1)S(1)} %bitcast.23), channel_id=1, replica_groups=mesh['y'=4,'zr'=8,'zl'=2,'x'=4,'c'=2] {'y','zl','x','c'}, dimensions={0} | all-to-all | bytes 2097152 | tf_op jit(solution)/shard_map/all_to_all | solution.py:33
  58.2 0.0 copy-done.1
  58.2 0.9 project.1
  59.1 14.5 %all_to_all.52 = bf16[8,72,512]{2,1,0:T(8,128)(2,1)S(1)} all-to-all(bf16[8,72,512]{2,1,0:T(8,128)(2,1)S(1)} %bitcast.21), channel_id=1, replica_groups=mesh['y'=4,'zr'=8,'zl'=2,'x'=4,'c'=2] {'c','x'}, dimensions={0} | all-to-all | bytes 1179648 | tf_op jit(solution)/shard_map/all_to_all | solution.py:33
  73.6 0.1 reduce_sum.12
  73.8 14.7 %all_to_all.53.both = bf16[8,88,512]{2,1,0:T(8,128)(2,1)S(1)} all-to-all(bf16[8,88,512]{2,1,0:T(8,128)(2,1)S(1)} %broadcast_in_dim.24), channel_id=1, replica_groups=mesh['y'=4,'zr'=8,'zl'=2,'x'=4,'c'=2] {'c','x'}, dimensions={0} | all-to-all | bytes 1441792 | tf_op jit(solution)/shard_map/all_to_all | solution.py:33
  88.5 0.0 copy-done
  88.5 1.4 convolution_convert_fusion
  89.9 22.5 %all_to_all.54.parts = bf16[8,64,1408]{2,1,0:T(8,128)(2,1)S(1)} all-to-all(bf16[8,64,1408]{2,1,0:T(8,128)(2,1)S(1)} %bitcast.24), channel_id=1, replica_groups=mesh['y'=4,'zr'=8,'zl'=2,'x'=4,'c'=2] {'zl','y'}, dimensions={0} | all-to-all | bytes 2883584 | tf_op jit(solution)/shard_map/all_to_all | solution.py:33
  112.4 0.0 copy-start.3
  112.4 0.0 copy-start.4
  112.4 0.2 near_sum.1
  112.6 18.3 %all_to_all.55.parts = bf16[8,8,1408]{2,1,0:T(8,128)(2,1)S(1)} all-to-all(bf16[8,8,1408]{2,1,0:T(8,128)(2,1)S(1)} %bitcast.22), channel_id=1, replica_groups=mesh['y'=4,'zr'=8,'zl'=2,'x'=4,'c'=2] {'zr'}, dimensions={0} | all-to-all | bytes 360448 | tf_op jit(solution)/shard_map/all_to_all | solution.py:33
  131.0 0.1 own_sum.1
  131.0 12.3 %all_to_all.56.parts = f32[32,1,128]{2,1,0:T(1,128)S(1)} all-to-all(f32[32,1,128]{2,1,0:T(1,128)S(1)} %get-tuple-element.10), channel_id=1, replica_groups=mesh['y'=4,'zr'=8,'zl'=2,'x'=4,'c'=2] {'y','x','c'}, dimensions={0} | all-to-all | bytes 32768 | tf_op jit(solution)/shard_map/all_to_all | solution.py:33
  143.4 15.0 %all_to_all.57.square = f32[16,1,128]{2,1,0:T(1,128)S(1)} all-to-all(f32[16,1,128]{2,1,0:T(1,128)S(1)} %plane_sum.1), channel_id=1, replica_groups=mesh['y'=4,'zr'=8,'zl'=2,'x'=4,'c'=2] {'zr','zl'}, dimensions={0} | all-to-all | bytes 16384 | tf_op jit(solution)/shard_map/all_to_all | solution.py:33
  158.4 0.0 copy-done.3
  158.4 0.0 copy-done.4
  158.4 0.2 adam.1
  158.5 19.0 %all_to_all.58 = bf16[8,8,1408]{2,1,0:T(8,128)(2,1)S(1)} all-to-all(bf16[8,8,1408]{2,1,0:T(8,128)(2,1)S(1)} %adam.1), channel_id=1, replica_groups=mesh['y'=4,'zr'=8,'zl'=2,'x'=4,'c'=2] {'zr'}, dimensions={0} | all-to-all | bytes 360448 | tf_op jit(solution)/shard_map/all_to_all | solution.py:33
  177.6 0.1 broadcast_in_dim.25
  177.7 0.0 copy-start.2
  177.7 19.7 %all_to_all.59 = bf16[8,64,1408]{2,1,0:T(8,128)(2,1)S(1)} all-to-all(bf16[8,64,1408]{2,1,0:T(8,128)(2,1)S(1)} %broadcast_in_dim.25), channel_id=1, replica_groups=mesh['y'=4,'zr'=8,'zl'=2,'x'=4,'c'=2] {'zl','y'}, dimensions={0} | all-to-all | bytes 2883584 | tf_op jit(solution)/shard_map/all_to_all | solution.py:33
  197.4 0.0 copy-done.2
  197.4 1.2 apply_update.1
  (7 shorter events, 0.2 us)
Async XLA Ops:
  0.6 87.9 %copy-start = (bf16[576,1408]{1,0:T(8,128)(2,1)S(1)}, bf16[576,1408]{1,0:T(8,128)(2,1)}, u32[]{:S(2)}) copy-start(bf16[576,1408]{1,0:T(8,128)(2,1)} %param.7) | copy-start | bytes 4866052
  36.0 22.2 %copy-start.1 = (bf16[576,1024]{1,0:T(8,128)(2,1)S(1)}, bf16[576,1024]{1,0:T(8,128)(2,1)}, u32[]{:S(2)}) copy-start(bf16[576,1024]{1,0:T(8,128)(2,1)} %inputs.1) | copy-start | bytes 3538948
  112.4 45.9 %copy-start.3 = (f32[8,1408]{1,0:T(8,128)S(1)}, f32[8,1408]{1,0:T(8,128)}, u32[]{:S(2)}) copy-start(f32[8,1408]{1,0:T(8,128)} %first_moment.3) | copy-start | bytes 135172
  112.4 45.9 %copy-start.4 = (f32[8,1408]{1,0:T(8,128)S(1)}, f32[8,1408]{1,0:T(8,128)}, u32[]{:S(2)}) copy-start(f32[8,1408]{1,0:T(8,128)} %second_moment.3) | copy-start | bytes 135172
  177.7 19.8 %copy-start.2 = (bf16[128,1408]{1,0:T(8,128)(2,1)S(1)}, bf16[128,1408]{1,0:T(8,128)(2,1)}, u32[]{:S(2)}) copy-start(bf16[128,1408]{1,0:T(8,128)(2,1)} %weight.1) | copy-start | bytes 1081348
